TPU v7x, 32 devices: a whole 2x2x4 slice. The times are simulated.
32 devices in a mesh: dp: 8 (over y, x, core), mp: 4 (over z).
Axes of the slice: x: 2, y: 2, z: 4, core: 2. Of those that a mesh axis runs over, the one named last changes fastest.
Arguments:
- hidden: bfloat16 [12288, 1024], P(('dp', 'mp')), may hold values from -6 to 6
- lengths: int32 [8], P('dp'), may hold values from 1 to 1536, 7372 in all
- first_gain: float32 [1024], replicated, may hold values from 0.5 to 1.5
- first_shift: float32 [1024], replicated, may hold values from -1.75 to 1.75
- projection_in: bfloat16 [1024, 3, 1024], P(None, None, 'mp'), may hold values from -0.1875 to 0.1875
- query_value_bias: float32 [2, 1024], P(None, 'mp'), may hold values from -0.625 to 0.625
- projection_out: bfloat16 [1024, 1024], P('mp'), may hold values from -2 to 2
- out_bias: float32 [1024], replicated, may hold values from -1.75 to 1.75
- second_gain: float32 [1024], replicated, may hold values from 0.5 to 1.5
- second_shift: float32 [1024], replicated, may hold values from -1.75 to 1.75
- up_weight: bfloat16 [1024, 4096], P(None, 'mp'), may hold values from -0.1875 to 0.1875
- up_bias: bfloat16 [4096], P('mp'), may hold values from -1.75 to 1.75
- down_weight: bfloat16 [4096, 1024], P('mp'), may hold values from -0.09375 to 0.09375
- down_bias: float32 [1024], replicated, may hold values from -1.75 to 1.75
- cotangent: bfloat16 [12288, 1024], P(('dp', 'mp')), may hold values from -6 to 6
Outputs:
- output: bfloat16 [12288, 1024], P(('dp', 'mp'))
- gradient_hidden: bfloat16 [12288, 1024], P(('dp', 'mp'))
- gradient_first_gain: float32 [1024], replicated
- gradient_first_shift: float32 [1024], replicated
- gradient_projection_in: float32 [1024, 3, 1024], P('dp', None, 'mp')
- gradient_query_value_bias: float32 [2, 1024], replicated
- gradient_projection_out: float32 [1024, 1024], P('mp', 'dp')
- gradient_out_bias: float32 [1024], replicated
- gradient_second_gain: float32 [1024], replicated
- gradient_second_shift: float32 [1024], replicated
- gradient_up_weight: float32 [1024, 4096], P('dp', 'mp')
- gradient_up_bias: float32 [4096], replicated
- gradient_down_weight: float32 [4096, 1024], P('mp', 'dp')
- gradient_down_bias: float32 [1024], replicated
Inputs may be any that keep to these rules, and one draw needn't show every extreme that they name: `lengths`: each utterance has at least one frame and at most 1536; the longest has exactly 1536.
All inputs are finite; a program needn't handle non-finite values. No bound on the sum of `lengths` on one device may be relied on, other than what follows from the above.
Results may differ from a plain program's by a relative error of at most 0.019.
Values may be sent and summed in bfloat16 or wider, within the bound.
No kernel may reach another device: no remote copies, remote signals or barrier semaphores. Data moves between devices by JAX's collectives and lax.ppermute only.
A program may use at most 128 MiB of HBM per device.

v0:
```python
import functools

import jax
import jax.numpy as jnp
from jax import lax
from jax.experimental import pallas as pl
from jax.experimental.pallas import tpu as pltpu
from jax.sharding import PartitionSpec as P


HEAD_DIM = 64
TILE = 256
ROWS = 384
NEGATIVE = -1e30
EPS = 1e-05
LOW = jnp.bfloat16
WIDE = jnp.float32


def mm(left, right):
    return jnp.dot(left, right, preferred_element_type=WIDE)


def over_rows(left, right):
    return lax.dot_general(left, right, (((0,), (0,)), ((), ())), preferred_element_type=WIDE)


def over_cols(left, right):
    return lax.dot_general(left, right, (((1,), (1,)), ((), ())), preferred_element_type=WIDE)


def normalize(values):
    centered = values - jnp.mean(values, -1, keepdims=True)
    inverse = lax.rsqrt(jnp.mean(centered * centered, -1, keepdims=True) + EPS)
    return (centered * inverse, inverse)


def norm_back(incoming, scaled_in, inverse, gain):
    weighted = incoming * gain
    return inverse * (
        weighted
        - jnp.mean(weighted, -1, keepdims=True)
        - scaled_in * jnp.mean(weighted * scaled_in, -1, keepdims=True)
    )


def split_three(value):
    high = value.astype(LOW)
    rest = value - high.astype(WIDE)
    low = rest.astype(LOW)
    return high, low, (rest - low.astype(WIDE)).astype(LOW)


def in_vmem():
    return pl.BlockSpec(memory_space=pltpu.VMEM)


def in_smem():
    return pl.BlockSpec(memory_space=pltpu.SMEM)


def shaped(shape, kind):
    return jax.ShapeDtypeStruct(shape, kind)


def params(mebibytes=40):
    return pltpu.CompilerParams(vmem_limit_bytes=mebibytes << 20)


SHARD, CHIP, LENGTH, HOME = 0, 1, 2, 3


def offset(place_ref, slot, size):
    return pl.multiple_of((place_ref[SHARD] ^ slot) * size, size)


def open_kernel(blocks, place_ref, scale_ref, bias_ref, local_ref, out_ref, *refs):
    pieces, refs = refs[:blocks], refs[blocks:]
    members = (len(refs) - 4) // 2
    firsts, parts, (weights_ref, turned_ref, out_copy, sems) = refs[:members], refs[members : 2 * members], refs[2 * members :]
    size, part = pieces[0].shape[0], local_ref.shape[2]
    at_home = place_ref[HOME] == 1

    def copies(action):
        @pl.when(at_home)
        def _():
            for at in range(3):
                to = weights_ref.at[:, at * part : (at + 1) * part]
                getattr(pltpu.make_async_copy(local_ref.at[at], to, sems.at[0, at]), action)()
            getattr(pltpu.make_async_copy(out_ref, out_copy, sems.at[1, 0]), action)()

        @pl.when(jnp.logical_not(at_home))
        def _():
            for block, piece in enumerate(pieces):
                some = pl.ds(pl.multiple_of((place_ref[CHIP] ^ block) * size, size), size)
                getattr(pltpu.make_async_copy(piece.at[:, : 3 * part], weights_ref.at[some, :], sems.at[0, block]), action)()
                getattr(pltpu.make_async_copy(piece.at[:, 3 * part :], turned_ref.at[some, :], sems.at[1, block]), action)()

    copies("start")
    copies("wait")

    @pl.when(at_home)
    def _():
        turned_ref[...] = out_copy[...].T

    for first, out in zip(firsts, parts):
        out[...] = (mm(first[...], weights_ref[...]) * scale_ref[...] + bias_ref[...]).astype(LOW)


def open_up(place, local, out, scale, bias, pieces, firsts):
    rows, width = firsts[0].shape
    part = local.shape[2]
    anywhere = pl.BlockSpec(memory_space=pltpu.HBM)
    return pl.pallas_call(
        functools.partial(open_kernel, len(pieces)),
        in_specs=[in_smem()] + [in_vmem()] * 2 + [anywhere] * (2 + len(pieces)) + [in_vmem()] * len(firsts),
        out_specs=[in_vmem()] * (len(firsts) + 2),
        out_shape=[shaped((rows, 3 * part), LOW)] * len(firsts) + [shaped((width, 3 * part), LOW), shaped((width, part), LOW)],
        scratch_shapes=[pltpu.VMEM((part, width), LOW), pltpu.SemaphoreType.DMA((2, max(3, len(pieces))))],
        compiler_params=params(24),
        cost_estimate=pl.CostEstimate(flops=24 * rows * width * part, bytes_accessed=16 * width * part, transcendentals=0),
        name="open_up",
    )(place, scale, bias, local, out, *pieces, *firsts)


def attend_kernel(place_ref, *refs):
    members = (len(refs) - 6) // 2
    parts, refs = refs[:members], refs[members:]
    turned_ref, total_ref, outs = refs[0], refs[1], refs[2 : 2 + members]
    q_turned, v_turned, keys, keys_at, out_turned = refs[2 + members :]
    rows, width = keys.shape
    count = rows // members
    heads = width // HEAD_DIM
    length = place_ref[LENGTH]
    for slot, part in enumerate(parts):
        at = offset(place_ref, slot, count)
        q_turned[:, pl.ds(at, count)] = part[:, :width].T
        keys[pl.ds(at, count), :] = part[:, width : 2 * width]
        v_turned[:, pl.ds(at, count)] = part[:, 2 * width :].T
    key_row = lax.broadcasted_iota(jnp.int32, (rows, width), 0)
    lane = lax.broadcasted_iota(jnp.int32, (rows, width), 1)
    feature = lax.broadcasted_iota(jnp.int32, (width, TILE), 0)
    key_at = lax.broadcasted_iota(jnp.int32, (TILE, TILE), 0)
    query_at = lax.broadcasted_iota(jnp.int32, (TILE, TILE), 1)

    def one_head(head, _):
        first = pl.multiple_of(head * HEAD_DIM, HEAD_DIM)
        spare = lax.rem(head + 1, heads) * HEAD_DIM
        off = jnp.where(key_row < length, 0.0, NEGATIVE).astype(LOW)
        keys_at[...] = jnp.where(lane == spare, off, keys[...])

        def product(tile):
            query = q_turned[:, tile * TILE : (tile + 1) * TILE]
            query = jnp.where(feature // HEAD_DIM == head, query, jnp.where(feature == spare, 1.0, 0.0).astype(LOW))
            return mm(keys_at[: (tile + 1) * TILE, :], query)

        later = product(0)
        for tile in range(rows // TILE):
            cols = slice(tile * TILE, (tile + 1) * TILE)
            upto = (tile + 1) * TILE
            scores = later
            if upto < rows:
                later = product(tile + 1)
            last = jnp.where(key_at <= query_at, scores[tile * TILE :], NEGATIVE)
            highest = jnp.max(last, 0, keepdims=True)
            if tile:
                highest = jnp.maximum(highest, jnp.max(scores[: tile * TILE], 0, keepdims=True))
            weights = jnp.exp(last - highest)
            total = jnp.sum(weights, 0, keepdims=True)
            low = weights.astype(LOW)
            if tile:
                before = jnp.exp(scores[: tile * TILE] - highest)
                total = total + jnp.sum(before, 0, keepdims=True)
                low = jnp.concatenate([before.astype(LOW), low], 0)
            out = mm(v_turned[pl.ds(first, HEAD_DIM), :upto], low)
            out_turned[pl.ds(first, HEAD_DIM), cols] = out / total
            total_ref[pl.ds(head, 1), cols] = highest + jnp.log(total)
        return 0

    lax.fori_loop(0, heads, one_head, 0)
    turned_ref[...] = out_turned[...].astype(LOW)
    for slot, out in enumerate(outs):
        out[...] = out_turned[:, pl.ds(offset(place_ref, slot, count), count)].T.astype(LOW)


def attend(place, parts):
    members = len(parts)
    count, width = parts[0].shape[0], parts[0].shape[1] // 3
    rows = members * count
    return pl.pallas_call(
        attend_kernel,
        out_shape=[shaped((width, rows), LOW), shaped((8, rows), WIDE)] + [shaped((count, width), LOW)] * members,
        in_specs=[in_smem()] + [in_vmem()] * members,
        out_specs=[in_vmem()] * (2 + members),
        scratch_shapes=[
            pltpu.VMEM((width, rows), LOW),
            pltpu.VMEM((width, rows), LOW),
            pltpu.VMEM((rows, width), LOW),
            pltpu.VMEM((rows, width), LOW),
            pltpu.VMEM((width, rows), WIDE),
        ],
        compiler_params=params(32),
        cost_estimate=pl.CostEstimate(flops=16 * rows * rows * width, bytes_accessed=8 * rows * width, transcendentals=rows * rows * 2),
        name="attend",
    )(place, *parts)


def attend_back_kernel(place_ref, *refs):
    members = (len(refs) - 17) // 2
    parts, grads, refs = refs[:members], refs[members : 2 * members], refs[2 * members :]
    turned_ref, total_ref, out_ref = refs[:3]
    (queries, keys, values, grad, q_turned, k_turned, g_turned, q_side, g_side, q_head, g_head, dq_turned, dk_sum, dv_sum) = refs[3:]
    rows, width = keys.shape
    count = rows // members
    heads = width // HEAD_DIM
    length = place_ref[LENGTH]
    for slot, (part, piece) in enumerate(zip(parts, grads)):
        at = offset(place_ref, slot, count)
        some = pl.ds(at, count)
        queries[some, :] = part[:, :width]
        keys[some, :] = part[:, width : 2 * width]
        values[some, :] = part[:, 2 * width :]
        grad[some, :] = piece[...]
        q_turned[:, some] = part[:, :width].T
        k_turned[:, some] = part[:, width : 2 * width].T
        g_turned[:, some] = piece[...].T
    dk_sum[...] = jnp.zeros_like(dk_sum)
    dv_sum[...] = jnp.zeros_like(dv_sum)
    lane_all = lax.broadcasted_iota(jnp.int32, (rows, width), 1)
    feature = lax.broadcasted_iota(jnp.int32, (width, rows), 0)
    lane = lax.broadcasted_iota(jnp.int32, (TILE, width), 1)
    key_at = lax.broadcasted_iota(jnp.int32, (TILE, TILE), 0)
    query_at = lax.broadcasted_iota(jnp.int32, (TILE, TILE), 1)
    none, one = jnp.zeros((), LOW), jnp.ones((), LOW)

    def one_head(head, _):
        first = pl.multiple_of(head * HEAD_DIM, HEAD_DIM)
        mine = pl.ds(first, HEAD_DIM)
        spare = lax.rem(head + 1, heads) * HEAD_DIM
        total = total_ref[pl.ds(head, 1), :]
        inner = jnp.sum(g_turned[mine, :].astype(WIDE) * turned_ref[mine, :].astype(WIDE), 0, keepdims=True)
        held = feature // HEAD_DIM == head

        def side(turned, taken, fourth):
            high, low, least = split_three(-taken)
            extra = jnp.where(feature == spare, high, jnp.where(feature == spare + 1, low, jnp.where(feature == spare + 2, least,
                jnp.where(feature == spare + 3, fourth, none))))
            return jnp.where(held, turned, extra)

        q_side[...] = side(q_turned[...], total, one)
        g_side[...] = side(g_turned[...], inner, none)
        own = lane_all // HEAD_DIM == head
        q_head[...] = jnp.where(own, queries[...], none)
        g_head[...] = jnp.where(own, grad[...], none)

        def products(start):
            at = slice(start, start + TILE)
            key_row = lax.broadcasted_iota(jnp.int32, (TILE, width), 0) + start
            off = jnp.where(key_row < length, 0.0, NEGATIVE).astype(LOW)
            ones = (lane >= spare) & (lane < spare + 3)
            scores = mm(jnp.where(ones, one, jnp.where(lane == spare + 3, off, keys[at, :])), q_side[:, start:])
            return scores, mm(jnp.where(ones, one, values[at, :]), g_side[:, start:])

        later = products(0)
        for tile in range(rows // TILE):
            start = tile * TILE
            at = slice(start, start + TILE)
            scores, back = later
            if start + TILE < rows:
                later = products(start + TILE)
            weights = jnp.exp(scores)
            near = jnp.where(key_at <= query_at, weights[:, :TILE], 0.0)
            weights = jnp.concatenate([near, weights[:, TILE:]], 1) if start + TILE < rows else near
            back_scores = (weights * back).astype(LOW)
            dv_sum[at, :] += mm(weights.astype(LOW), g_head[start:, :])
            dk_sum[at, :] += mm(back_scores, q_head[start:, :])
            dq = mm(k_turned[mine, at], back_scores)
            if tile:
                dq_turned[mine, start:] += dq
            else:
                dq_turned[mine, :] = dq
        return 0

    lax.fori_loop(0, heads, one_head, 0)
    for slot in range(members):
        some = pl.ds(offset(place_ref, slot, count), count)
        to = slice(slot * count, (slot + 1) * count)
        dq = dq_turned[:, some].T.astype(LOW).astype(WIDE)
        out_ref[to, :width] = (dq * HEAD_DIM**-0.5).astype(LOW)
        out_ref[to, width : 2 * width] = dk_sum[some, :].astype(LOW)
        out_ref[to, 2 * width :] = dv_sum[some, :].astype(LOW)


def attend_back(place, parts, grads, turned, total):
    members = len(parts)
    count, width = parts[0].shape[0], parts[0].shape[1] // 3
    rows = members * count
    low = lambda *shape: pltpu.VMEM(shape, LOW)
    wide = lambda *shape: pltpu.VMEM(shape, WIDE)
    return pl.pallas_call(
        attend_back_kernel,
        out_shape=shaped((rows, 3 * width), LOW),
        in_specs=[in_smem()] + [in_vmem()] * (2 * members + 2),
        out_specs=in_vmem(),
        scratch_shapes=[low(rows, width)] * 4 + [low(width, rows)] * 5 + [low(rows, width)] * 2
        + [wide(width, rows), wide(rows, width), wide(rows, width)],
        compiler_params=params(40),
        cost_estimate=pl.CostEstimate(flops=40 * rows * rows * width, bytes_accessed=20 * rows * width, transcendentals=rows * rows * 2),
        name="attend_back",
    )(place, *parts, *grads, turned, total)


def project_kernel(*refs):
    members = (len(refs) - 6) // 2
    parts, outs, refs = refs[:members], refs[members : 2 * members], refs[2 * members :]
    hidden_ref, bias_ref, gain_ref, shift_ref, middle_ref, second_ref = refs
    total = hidden_ref[...].astype(WIDE) + bias_ref[...]
    for part, out in zip(parts, outs):
        total = total + over_cols(part[...], out[...])
    middle_ref[...] = total
    second_ref[...] = (normalize(total)[0] * gain_ref[...] + shift_ref[...]).astype(LOW)


def project(parts, outs, hidden, bias, gain, shift):
    rows, width = hidden.shape
    return pl.pallas_call(
        project_kernel,
        out_shape=[shaped((rows, width), WIDE), shaped((rows, width), LOW)],
        in_specs=[in_vmem()] * (2 * len(parts) + 4),
        out_specs=[in_vmem()] * 2,
        compiler_params=params(24),
        cost_estimate=pl.CostEstimate(flops=2 * rows * width * width, bytes_accessed=2 * width * width + 10 * rows * width, transcendentals=rows),
        name="project",
    )(*parts, *outs, hidden, bias, gain, shift)


def feed_kernel(blocks, place_ref, x_one, x_two, g_one, g_two, bias_ref, up_local, down_local, *refs):
    pieces, refs = refs[:blocks], refs[blocks:]
    act_ref, back_ref, sums_ref, out_ref, grad_ref, other_ref, up_ref, down_ref, up_sems, down_sems = refs
    half, size = x_one.shape[0], pieces[0].shape[0] // 2
    at_home = place_ref[HOME] == 1

    def copies(action):
        @pl.when(at_home)
        def _():
            getattr(pltpu.make_async_copy(up_local, up_ref, up_sems.at[0]), action)()
            getattr(pltpu.make_async_copy(down_local, down_ref, down_sems.at[0]), action)()

        @pl.when(jnp.logical_not(at_home))
        def _():
            for block, piece in enumerate(pieces):
                some = pl.ds(pl.multiple_of((place_ref[CHIP] ^ block) * size, size), size)
                getattr(pltpu.make_async_copy(piece.at[:size, :], up_ref.at[some, :], up_sems.at[block]), action)()
                getattr(pltpu.make_async_copy(piece.at[size:, :], down_ref.at[some, :], down_sems.at[block]), action)()

    copies("start")
    copies("wait")
    sums = jnp.zeros(sums_ref.shape, WIDE)
    for which, (x_ref, g_ref) in enumerate(((x_one, g_one), (x_two, g_two))):
        for start in range(0, half, ROWS):
            at = slice(start, start + ROWS)
            to = slice(which * half + start, which * half + start + ROWS)
            before = mm(x_ref[at, :], up_ref[...]) + bias_ref[...]
            inside = 0.5 * (1.0 + lax.erf(before * 0.5**0.5))
            slope = inside + before * (jnp.exp(-0.5 * before * before) * (0.5 / jnp.pi) ** 0.5)
            act = (before * inside).astype(LOW)
            back = (over_cols(g_ref[at, :], down_ref[...]) * slope).astype(LOW)
            act_ref[to, :] = act
            back_ref[to, :] = back
            sums = sums + jnp.sum(back.astype(WIDE), 0, keepdims=True)
            out, grad = mm(act, down_ref[...]), over_cols(back, up_ref[...])
            if which:
                other_ref[at, :] = out.astype(LOW)
                other_ref[half + start : half + start + ROWS, :] = grad.astype(LOW)
            else:
                out_ref[at, :] = out.astype(out_ref.dtype)
                grad_ref[at, :] = grad.astype(grad_ref.dtype)
    sums_ref[...] = sums


def feed(place, x_one, x_two, g_one, g_two, bias, up, down, pieces, wide_first):
    half, width = x_one.shape
    hidden = up.shape[1]
    flat = [shaped((half, width), WIDE if wide_first else LOW)] * 2 + [shaped((2 * half, width), LOW)]
    return pl.pallas_call(
        functools.partial(feed_kernel, len(pieces)),
        in_specs=[in_smem()] + [in_vmem()] * 5 + [pl.BlockSpec(memory_space=pltpu.HBM)] * (2 + len(pieces)),
        out_specs=[in_vmem()] * 6,
        out_shape=[shaped((2 * half, hidden), LOW)] * 2 + [shaped((1, hidden), WIDE)] + flat,
        scratch_shapes=[pltpu.VMEM((width, hidden), LOW), pltpu.VMEM((hidden, width), LOW)]
        + [pltpu.SemaphoreType.DMA((len(pieces),))] * 2,
        compiler_params=params(40),
        cost_estimate=pl.CostEstimate(flops=16 * half * width * hidden, bytes_accessed=4 * width * hidden, transcendentals=4 * half * hidden),
        name="feed",
    )(place, x_one, x_two, g_one, g_two, bias, up, down, *pieces)


def unproject_kernel(own_ref, mate_ref, near_ref, middle_ref, cotangent_ref, gain_ref, *refs):
    members = (len(refs) - 3) // 2
    weights, (low_ref, back_ref, sums_ref), outs = refs[:members], refs[members : members + 3], refs[members + 3 :]
    hat, inverse = normalize(middle_ref[...])
    second = own_ref[...] + mate_ref[own_ref.shape[0] :, :].astype(WIDE) + near_ref[...].astype(WIDE)
    cotangent = cotangent_ref[...].astype(WIDE)
    back = cotangent + norm_back(second, hat, inverse, gain_ref[...])
    low = back.astype(LOW)
    back_ref[...] = back
    low_ref[...] = low
    for weight, out in zip(weights, outs):
        out[...] = mm(low, weight[...]).astype(LOW)
    sums_ref[0:1, :] = jnp.sum(second * hat, 0, keepdims=True)
    sums_ref[1:2, :] = jnp.sum(second, 0, keepdims=True)
    sums_ref[2:3, :] = jnp.sum(back, 0, keepdims=True)
    sums_ref[3:4, :] = jnp.sum(cotangent, 0, keepdims=True)
    sums_ref[4:, :] = jnp.zeros_like(sums_ref[4:, :])


def unproject(own, mate, near, middle, cotangent, gain, outs):
    rows, width = own.shape
    members, part = len(outs), outs[0].shape[1]
    return pl.pallas_call(
        unproject_kernel,
        out_shape=[shaped((rows, width), LOW), shaped((rows, width), WIDE), shaped((8, width), WIDE)] + [shaped((rows, part), LOW)] * members,
        in_specs=[in_vmem()] * (6 + members),
        out_specs=[in_vmem()] * (3 + members),
        compiler_params=params(56),
        cost_estimate=pl.CostEstimate(flops=2 * rows * width * width, bytes_accessed=2 * width * width + 18 * rows * width, transcendentals=rows),
        name="unproject",
    )(own, mate, near, middle, cotangent, gain, *outs)


def weigh_kernel(place_ref, *refs):
    pairs = (len(refs) - 6) // 6
    xs, gs, refs = refs[: 2 * pairs], refs[2 * pairs : 4 * pairs], refs[4 * pairs :]
    acts, backs, refs = refs[:pairs], refs[pairs : 2 * pairs], refs[2 * pairs :]
    up_keep, up_send, down_keep, down_send, x_turned, g_turned = refs
    count = xs[0].shape[0]
    blocks, size = 2 * up_keep.shape[0], up_keep.shape[1]
    for at, (x, g) in enumerate(zip(xs, gs)):
        x_turned[:, at * count : (at + 1) * count] = x[...].T
        g_turned[:, at * count : (at + 1) * count] = g[...].T
    for block in range(blocks):
        some = pl.ds(pl.multiple_of((place_ref[CHIP] ^ block) * size, size), size)
        product = lambda turned, parts: sum(mm(turned[some, at * 2 * count : (at + 1) * 2 * count], part[...]) for at, part in enumerate(parts))
        to = up_send if block % 2 else up_keep
        to[block // 2] = product(x_turned, backs).astype(LOW)
        to = down_send if block >= blocks // 2 else down_keep
        to[block % (blocks // 2)] = product(g_turned, acts).astype(LOW)


def weigh(place, xs, gs, acts, backs, chips):
    count, width = xs[0].shape
    hidden = acts[0].shape[1]
    rows = len(xs) * count
    return pl.pallas_call(
        weigh_kernel,
        in_specs=[in_smem()] + [in_vmem()] * (2 * len(xs) + 2 * len(acts)),
        out_specs=[in_vmem()] * 4,
        out_shape=[shaped((chips // 2, width // chips, hidden), LOW)] * 4,
        scratch_shapes=[pltpu.VMEM((width, rows), LOW)] * 2,
        compiler_params=params(40),
        cost_estimate=pl.CostEstimate(flops=4 * rows * width * hidden, bytes_accessed=4 * width * hidden + 8 * rows * width, transcendentals=0),
        name="weigh",
    )(place, *xs, *gs, *acts, *backs)


def turn_kernel(*refs):
    out = refs[-1]
    for at, ref in enumerate(refs[:-1]):
        count = ref.shape[0]
        out[:, at * count : (at + 1) * count] = ref[...].T


def turn(parts):
    count, width = parts[0].shape
    return pl.pallas_call(
        turn_kernel,
        in_specs=[in_vmem()] * len(parts),
        out_specs=in_vmem(),
        out_shape=shaped((width, len(parts) * count), LOW),
        compiler_params=params(40),
        cost_estimate=pl.CostEstimate(flops=0, bytes_accessed=4 * len(parts) * count * width, transcendentals=0),
        name="turn",
    )(*parts)


def weigh_late_kernel(place_ref, turned_ref, projected_ref, weight_ref, context_ref, *refs):
    members = len(refs) - 7
    lows, (one_keep, one_send, two_keep, two_send, gain_ref, sums_ref, out_turned) = refs[:members], refs[members:]
    count = lows[0].shape[0]
    blocks, size, cols = 2 * one_keep.shape[0], one_keep.shape[1], one_keep.shape[2]
    out = sum(mm(context_ref[:, pl.ds(offset(place_ref, slot, count), count)], low[...]) for slot, low in enumerate(lows))
    out_turned[...] = out.T.astype(LOW)
    sums = jnp.sum(projected_ref[...].astype(WIDE), 0, keepdims=True)
    sums_ref[...] = sums
    for block in range(blocks):
        some = pl.ds(pl.multiple_of((place_ref[CHIP] ^ block) * size, size), size)
        product = mm(turned_ref[some, :], projected_ref[...])
        weight = weight_ref[some, : product.shape[1]].astype(WIDE)
        gain = jnp.sum(product * weight, 1, keepdims=True)
        shift = jnp.sum(sums * weight, 1, keepdims=True)
        lane = lax.broadcasted_iota(jnp.int32, (size, gain_ref.shape[1]), 1)
        gain_ref[some, :] = jnp.where(lane == 0, gain, shift)
        to = one_send if block % 2 else one_keep
        to[block // 2] = product[:, :cols].astype(LOW)
        to = two_send if block >= blocks // 2 else two_keep
        rest = product.shape[1] - cols
        to[block % (blocks // 2), :, :rest] = product[:, cols:].astype(LOW)
        to[block % (blocks // 2), :, rest:] = out_turned[some, :]


def weigh_late(place, turned, projected, weight, context, lows, chips):
    width, rows = turned.shape
    part = context.shape[0]
    cols = 2 * part
    return pl.pallas_call(
        weigh_late_kernel,
        in_specs=[in_smem()] + [in_vmem()] * (4 + len(lows)),
        out_specs=[in_vmem()] * 6,
        out_shape=[shaped((chips // 2, width // chips, cols), LOW)] * 4
        + [shaped((width, 128), WIDE), shaped((1, 3 * part), WIDE)],
        scratch_shapes=[pltpu.VMEM((width, part), LOW)],
        compiler_params=params(32),
        cost_estimate=pl.CostEstimate(flops=8 * rows * width * part, bytes_accessed=4 * rows * width + 12 * width * part, transcendentals=0),
        name="weigh_late",
    )(place, turned, projected, weight, context, *lows)


def share_kernel(projected_ref, weight_ref, zero_ref, one_ref, high_ref):
    count = zero_ref.shape[0]
    high_ref[...] = over_cols(projected_ref[2 * count :, :], weight_ref[...]).astype(LOW)
    one_ref[...] = over_cols(projected_ref[count : 2 * count, :], weight_ref[...]).astype(LOW)
    zero_ref[...] = over_cols(projected_ref[:count, :], weight_ref[...])


def share(projected, weight):
    rows, width = projected.shape[0], weight.shape[0]
    return pl.pallas_call(
        share_kernel,
        in_specs=[in_vmem()] * 2,
        out_specs=[in_vmem()] * 3,
        out_shape=[shaped((rows // 4, width), WIDE), shaped((rows // 4, width), LOW), shaped((rows // 2, width), LOW)],
        compiler_params=params(40),
        cost_estimate=pl.CostEstimate(flops=2 * rows * width * weight.shape[1], bytes_accessed=6 * rows * width, transcendentals=0),
        name="share",
    )(projected, weight)


def flip(size, bit):
    return [(at, at ^ bit) for at in range(size)]


def add_low(kept, taken):
    return (kept.astype(WIDE) + taken.astype(WIDE)).astype(LOW)


def add_up(values, axis, wide):
    size, bit = lax.axis_size(axis), 1
    while bit < size:
        mate = lax.ppermute(values, axis, flip(size, bit))
        if wide and 2 * bit < size:
            values = (values + mate) + (lax.ppermute(values, axis, flip(size, 2 * bit)) + lax.ppermute(values, axis, flip(size, 3 * bit)))
            bit *= 2
        else:
            values = values + mate
        bit *= 2
    return values

PLAN = {'first': (None, 1), 'notes': (None, 0), 'cotangent': (3, 6), 'second': (None, 3), 'pieces': (None, 2), 'outs': (None, 4), 'seconds': (None, 70), 'last': (None, 5), 'cotmate': (None, 7), 'cotnear': (None, 8), 'secnear': (None, 8), 'two': (11, 12), 'three': (11, None), 'fed': (None, 15), 'out': (None, 14), 'low': (None, 16), 'fedrest': (None, 16), 'hand': (None, 20), 'output': (None, 16), 'late': (None, 20), 'laterest': (None, 21), 'latehand': (None, None), 'early': 1, 'half': 1, 'sums': 19, 'middle': 20, 'wide': 0, 'lateend': 1}


class Box:
    def __init__(self, value=None, at=None):
        self.value, self.at = value, at


class Order:
    def __init__(self):
        self.boxes, self.later = [], {}

    def keep(self, value, at):
        box = Box(value, at)
        self.boxes.append(box)
        return box

    def point(self, at, *values):
        boxes = [box for box in self.boxes if box.at == at]
        if boxes:
            tied = lax.optimization_barrier((*values, *[box.value for box in boxes]))
            values = tied[: len(values)]
            for box, value in zip(boxes, tied[len(values) :]):
                box.value, box.at = value, None
        for action in self.later.pop(at, ()):
            action()
        return values if len(values) > 1 else values[0]

    def send(self, name, operand, move):
        start, end = PLAN[name]
        result = Box()

        def go():
            with jax.named_scope(name):
                result.value = move(operand.value)
            result.at = end
            self.boxes.append(result)

        if start is None:
            go()
        else:
            operand.at = start
            if operand not in self.boxes:
                self.boxes.append(operand)
            self.later.setdefault(start, []).append(go)
        return result


def body(hidden, lengths, first_gain, first_shift, projection_in, query_value_bias, projection_out, out_bias,
         second_gain, second_shift, up_weight, up_bias, down_weight, down_bias, cotangent):
    rows, width = hidden.shape
    heads_width = projection_in.shape[2]
    hidden_width = up_weight.shape[1]
    groups, members = lax.axis_size("dp"), lax.axis_size("mp")
    group, member = lax.axis_index("dp"), lax.axis_index("mp")
    chips = groups // 2
    core, chip = group % 2, group // 2
    size, count = width // chips, width // groups
    scale = HEAD_DIM ** (-0.5)
    at_home = core == member // 2
    shard = jnp.where(at_home, member, member ^ 2)
    both = ("dp", "mp")
    away = [(at * 2 + 1 - z // 2, z) for at in range(chips) for z in range(members)]
    spot = lambda dp, mp: dp * members + mp
    far_pairs = [(spot(d, z), spot(d ^ 1, z ^ 2)) for d, z in away]
    near_mate_pairs = [(spot(d, z), spot(d ^ 1, z ^ 1)) for d in range(groups) for z in range(members)]
    hand_pairs = [(spot(d, z), spot(d, z ^ 2)) for d, z in away] + [(spot(d ^ 1, z), spot(d, z)) for d, z in away]
    away_pairs = lambda bit: [(spot(d, z), spot(d ^ (2 * bit), z)) for d, z in away]
    far = lambda value: lax.ppermute(value, both, far_pairs)
    mate = lambda value: lax.ppermute(value, "dp", flip(groups, 1))
    near = lambda value: lax.ppermute(value, "mp", flip(members, 1))
    near_mate = lambda value: lax.ppermute(value, both, near_mate_pairs)
    cross = lambda bit: lambda value: lax.ppermute(value, "dp", flip(groups, 2 * bit))
    row = lambda vector: vector.reshape(1, -1)
    order = Order()
    keep, point, send = order.keep, order.point, order.send
    pick = lambda own, got: jnp.where(at_home, own, got)

    def spread(name, piece):
        return [piece] + [send(name, keep(piece.value, None), lambda value, block=block: lax.ppermute(value, both, away_pairs(block))) for block in range(1, chips)]

    block_of = lambda value, axis: lax.dynamic_slice_in_dim(value, chip * size, size, axis)
    first_piece = jnp.concatenate([block_of(projection_in, 0).reshape(size, -1), block_of(projection_out, 1).T], 1)
    notes = jnp.concatenate([query_value_bias.reshape(-1), up_bias.astype(WIDE), jnp.broadcast_to(lengths.astype(WIDE), (512,))])
    first_far = send("first", keep(first_piece, None), far)
    notes_far = send("notes", keep(notes.reshape(-1, 128), None), far)
    cotangent_far = send("cotangent", keep(cotangent, None), far)
    second_piece = jnp.concatenate([block_of(up_weight, 0), block_of(down_weight, 0)], 0)
    second_far = send("second", keep(second_piece, None), far)
    hidden_own = pick(hidden, point(0, far(hidden)))
    notes = pick(notes, notes_far.value.reshape(-1))
    qv_bias = notes[: 2 * heads_width].reshape(2, heads_width)
    up_bias_own = row(notes[2 * heads_width : 2 * heads_width + hidden_width])
    length = notes[-1].astype(jnp.int32)
    place = jnp.stack([shard, chip, length, at_home.astype(jnp.int32)]).astype(jnp.int32)
    first_hat, first_inverse = normalize(hidden_own.astype(WIDE))
    first_own = (first_hat * first_gain + first_shift).astype(LOW)
    zero = jnp.zeros((heads_width,), WIDE)
    bias_flat = row(jnp.concatenate([qv_bias[0] * scale, zero, qv_bias[1]]))
    scale_flat = row(jnp.concatenate([zero + scale, zero + 1.0, zero + 1.0]))

    first_own = point(1, first_own)
    first_pieces = spread("pieces", first_far)
    first_near, first_mate = point(2, near(first_own), mate(first_own))
    firsts = [first_own, first_near, first_mate, mate(first_near)]
    *parts, weight_flat, out_own = open_up(
        place, projection_in.transpose(1, 0, 2), projection_out, scale_flat, bias_flat, [piece.value for piece in first_pieces], firsts
    )

    parts[1], out_own = point(3, parts[1], out_own)
    out_near, out_mate = send("outs", keep(out_own, None), near), send("outs", keep(out_own, None), mate)
    out_own = out_own
    turned, total, *context = attend(place, parts)
    context[1], context[2], context[3] = point(4, context[1], context[2], context[3])
    if second_far.value is not None:
        second_pieces = spread("seconds", second_far)
    out_last = send("last", keep(out_near.value, None), mate)
    exchange = (lambda value: value, near, mate, near_mate)
    context = [move(part) for move, part in zip(exchange, context)]
    context[1], context[2], context[3] = point(5, context[1], context[2], context[3])
    outs = [out_own, out_near.value, out_mate.value, out_last.value]
    middle, second_own = project(context, outs, hidden_own, row(out_bias), row(second_gain), row(second_shift))

    second_own = point(6, second_own)
    cotangent_own = keep(pick(cotangent, cotangent_far.value), None)
    second_mate, cotangent_mate, second_own, cotangent_own.value = point(
        7, mate(second_own), mate(cotangent_own.value), second_own, cotangent_own.value
    )
    second_near = send("secnear", keep(second_own, None), near)
    cotangent_near = send("cotnear", keep(cotangent_own.value, None), near)
    second_mate = point(70, second_mate)
    fed_weights = (up_bias_own, up_weight, down_weight, [piece.value for piece in second_pieces])
    act_one, back_one, bias_one, out_zero, grad_zero, other_two = feed(
        place, second_own, second_mate, cotangent_own.value, cotangent_mate, *fed_weights, True
    )
    act_one, other_two = point(8, act_one, other_two)
    two_got = send("two", keep(other_two, None), mate)
    second_near.value, cotangent_near.value = point(9, second_near.value, cotangent_near.value)
    second_last, cotangent_last = mate(second_near.value), mate(cotangent_near.value)
    act_two, back_two, bias_two, out_one, grad_one, other_three = feed(
        place, second_near.value, second_last, cotangent_near.value, cotangent_last, *fed_weights, False
    )
    three_got = mate(point(10, other_three))
    grad_next = add_low(grad_one, three_got[rows:])
    grad_near = near(grad_next)
    second_keep, grad_next = point(11, second_own, grad_next)
    up_keep, up_send, down_keep, down_send = weigh(
        place,
        [second_keep, second_mate, second_near.value, second_last],
        [cotangent_own.value, cotangent_mate, cotangent_near.value, cotangent_last],
        [act_one, act_two],
        [back_one, back_two],
        chips,
    )
    up_got = send("fed", keep(up_send, None), cross(1))
    down_got = send("fed", keep(down_send, None), cross(chips // 2))
    grad_near, up_keep = point(12, grad_near, up_keep)
    low_middle, back_middle, sums_part, *back_context = unproject(
        grad_zero, two_got.value, grad_near, middle, cotangent_own.value, row(second_gain), outs
    )
    out_next = add_low(out_one, three_got[:rows])
    out_sum = send("out", keep(out_next, None), near)

    back_context[1], low_middle = point(13, back_context[1], low_middle)
    back_context = [move(part) for move, part in zip(exchange, back_context)]
    first_turned = keep(turn(firsts), 14)
    back_context[1], back_context[2], back_context[3], low_middle = point(14, back_context[1], back_context[2], back_context[3], low_middle)

    def halved(up_keep, up_got, down_keep, down_got):
        return add_low(up_keep, up_got), add_low(down_keep, down_got)

    def handed(name, value):
        rows_of = lambda at: lax.dynamic_slice_in_dim(value, at * count, count, 0)
        kept, given = rows_of(member // 2), rows_of(1 - member // 2)
        return kept, send(name, keep(kept, None), far), send(name, keep(given, None), lambda value: lax.ppermute(value, both, hand_pairs))

    settled = lambda kept, got_far, got: pick(kept, got_far.value).astype(WIDE) + got.value.astype(WIDE)
    low_mate, low_near = send("low", keep(low_middle, None), mate), send("low", keep(low_middle, None), near)
    written = lambda: (middle + out_zero + two_got.value[:rows].astype(WIDE) + out_sum.value.astype(WIDE) + down_bias).astype(LOW)
    if PLAN["early"]:
        output = keep(written(), 15)
    back_context[1], up_keep, down_keep = point(15, back_context[1], up_keep, down_keep)
    up_sum, down_sum = halved(up_keep, up_got.value, down_keep, down_got.value) if PLAN["half"] else (None, None)

    def rest(up_sum, down_sum, name):
        bit, sent = 2, []
        while bit < chips:
            half = down_sum.shape[0] // 2
            sent = send(name, keep(up_sum[1::2], None), cross(bit)), send(name, keep(down_sum[half:], None), cross(chips // 2 // bit))
            bit *= 2
            if bit < chips:
                up_sum, down_sum = halved(up_sum[0::2], sent[0].value, down_sum[:half], sent[1].value)
        return up_sum[0::2], sent[0], down_sum[: down_sum.shape[0] // 2], sent[1]

    def finish(up_keep, up_got, down_keep, down_got):
        up_sum, down_sum = halved(up_keep, up_got.value, down_keep, down_got.value)
        return jnp.concatenate([up_sum[0], down_sum[0]], 1)

    if PLAN["half"]:
        fed_rest = rest(up_sum, down_sum, "fedrest")
    if PLAN["early"]:
        output_far = send("output", keep(output.value, None), far)
    back_projected = attend_back(place, parts, back_context, turned, total)
    back_projected = point(16, back_projected)
    lows = [low_middle, low_near.value, low_mate.value, mate(low_near.value)]

    if not PLAN["half"]:
        up_sum, down_sum = halved(up_keep, up_got.value, down_keep, down_got.value)
        up_sum, back_projected = lax.optimization_barrier((up_sum, back_projected))
        fed_rest = rest(up_sum, down_sum, "fedrest")
    if PLAN["half"]:
        fed_sum = finish(*fed_rest)
        fed_sum, back_projected = lax.optimization_barrier((fed_sum, back_projected))
        fed_parts = handed("hand", fed_sum)
    share_zero, share_one, share_high = share(back_projected, weight_flat)
    share_high, back_projected = point(17, share_high, back_projected)
    share_got = mate(share_high)
    share_zero, share_next, back_projected = point(
        18, share_zero + share_got[:rows].astype(WIDE), add_low(share_one, share_got[rows:]), back_projected
    )
    share_near = near(share_next)
    *late_parts, late_gains, projected_sums = weigh_late(place, first_turned.value, back_projected, weight_flat, turned, lows, chips)
    late_parts[1], late_parts[3], share_zero = point(19, late_parts[1], late_parts[3], share_zero)
    late_up, late_down = send("late", keep(late_parts[1], None), cross(1)), send("late", keep(late_parts[3], None), cross(chips // 2))
    gains = keep(late_gains, PLAN["sums"])
    if not PLAN["early"]:
        output_far = send("output", keep(written(), None), far)
    if not PLAN["half"]:
        fed_parts = handed("hand", finish(*fed_rest))

    def gather_sums():
        placed = lambda value, whole: lax.dynamic_update_slice(jnp.zeros((whole,), WIDE), value, (shard * value.shape[0],))
        shift_grad = gains.value[:, 1]
        sums = [
            (gains.value[:, 0] - first_shift * shift_grad) / first_gain,
            shift_grad,
            placed(projected_sums[0, :heads_width], width),
            placed(projected_sums[0, 2 * heads_width :], width),
            sums_part[:4].reshape(-1),
            placed((bias_one + bias_two)[0], members * hidden_width),
        ]
        return add_up(jnp.concatenate(sums).reshape(-1, 128), "dp", PLAN["wide"])

    if PLAN["sums"] != 20:
        sums = keep(gather_sums(), PLAN["middle"])
    share_near, share_zero = point(20, share_near, share_zero)
    if PLAN["sums"] == 20:
        sums = keep(gather_sums(), PLAN["middle"])
    late_rest = rest(*halved(late_parts[0], late_up.value, late_parts[2], late_down.value), "laterest")
    if PLAN["lateend"] == 0:
        late_end = handed("latehand", finish(*late_rest))
    back_first = share_zero + share_near.astype(WIDE)
    hidden_grad = (back_middle + norm_back(back_first, first_hat, first_inverse, first_gain)).astype(LOW)
    hidden_grad = point(21, hidden_grad)
    hidden_grad_far = far(hidden_grad)
    if PLAN["lateend"] == 1:
        late_end = handed("latehand", finish(*late_rest))
    sums = add_up(sums.value, "mp", PLAN["wide"]).reshape(-1)
    fed_grad, late_grad = settled(*fed_parts), settled(*late_end)
    small = [sums[at * width : (at + 1) * width] for at in range(8)]
    return (
        pick(output.value if PLAN["early"] else written(), output_far.value),
        pick(hidden_grad, hidden_grad_far),
        small[0],
        small[1],
        late_grad[:, : 3 * heads_width].reshape(-1, 3, heads_width),
        sums[2 * width : 4 * width].reshape(2, width),
        late_grad[:, 3 * heads_width :].T,
        small[6],
        small[4],
        small[5],
        fed_grad[:, :hidden_width],
        sums[8 * width :],
        fed_grad[:, hidden_width:].T,
        small[7],
    )


def solution(mesh):
    placed = (
        P(("dp", "mp"), None),
        P("dp"),
        P(),
        P(),
        P(None, None, "mp"),
        P(None, "mp"),
        P("mp", None),
        P(),
        P(),
        P(),
        P(None, "mp"),
        P("mp"),
        P("mp", None),
        P(),
        P(("dp", "mp"), None),
    )
    return jax.shard_map(
        body,
        mesh=mesh,
        in_specs=placed,
        out_specs=(
            P(("dp", "mp"), None),
            P(("dp", "mp"), None),
            P(),
            P(),
            P("dp", None, "mp"),
            P(),
            P("mp", "dp"),
            P(),
            P(),
            P(),
            P("dp", "mp"),
            P(),
            P("mp", "dp"),
            P(),
        ),
        check_vma=False,
    )
```

profile of v0, /device:TPU:1, one launch (start us, length us, event | category | flops | bytes accessed | tf_op | source)
XLA Modules:
  0.0 351.4 jit_solution(17299443572540150036)
XLA Ops:
  0.6 5.6 %collective-permute-start = (bf16[384,1024]{1,0:T(8,128)(2,1)}, bf16[384,1024]{1,0:T(8,128)(2,1)S(1)}, u32[]{:S(2)}, u32[]{:S(2)}) collective-permute-start(bf16[384,1024]{1,0:T(8,128)(2,1)} %param.15), channel_id=1, source_target_pairs={{4,2},{5,3},{2,4},{3,5},{12,10},{13,11},{10,12},{11,13},{20,18},{2... | collective-permute-start | bytes 2359304 | tf_op jit(solution)/shard_map/ppermute | solution.py:636
  8.3 1.9 collective-permute-start.1
  12.7 4.5 %collective-permute-start.2 = (bf16[256,1024]{1,0:T(8,128)(2,1)S(1)}, bf16[256,1024]{1,0:T(8,128)(2,1)S(1)}, u32[]{:S(2)}, u32[]{:S(2)}) collective-permute-start(bf16[256,1024]{1,0:T(8,128)(2,1)S(1)} %pad_maximum_fusion.2), channel_id=1, source_target_pairs={{4,2},{5,3},{2,4},{3,5},{12,10},{13,11},{10,12},{11,13},{20,18},{2... | collective-permute-start | bytes 1572872 | tf_op jit(solution)/shard_map/first/ppermute | solution.py:636
  17.3 11.4 %collective-permute-done.1 = f32[16,128]{1,0:T(8,128)S(1)} collective-permute-done((f32[16,128]{1,0:T(8,128)S(1)}, f32[16,128]{1,0:T(8,128)S(1)}, u32[]{:S(2)}, u32[]{:S(2)}) %collective-permute-start.1) | collective-permute-done | bytes 8224 | tf_op jit(solution)/shard_map/notes/ppermute | solution.py:636
  29.8 6.2 %collective-permute-done.2.refs_0_ = bf16[256,1024]{1,0:T(8,128)(2,1)S(1)} collective-permute-done((bf16[256,1024]{1,0:T(8,128)(2,1)S(1)}, bf16[256,1024]{1,0:T(8,128)(2,1)S(1)}, u32[]{:S(2)}, u32[]{:S(2)}) %collective-permute-start.2) | collective-permute-done | bytes 524320 | tf_op jit(solution)/shard_map/first/ppermute | solution.py:636
  36.4 3.1 collective-permute-start.5
  39.5 3.1 collective-permute-start.6
  42.7 2.1 collective-permute-start.7
  47.9 6.4 %collective-permute-start.9 = (bf16[512,1024]{1,0:T(8,128)(2,1)}, bf16[512,1024]{1,0:T(8,128)(2,1)}, u32[]{:S(2)}, u32[]{:S(2)}) collective-permute-start(bf16[512,1024]{1,0:T(8,128)(2,1)} %pad_maximum_fusion), channel_id=1, source_target_pairs={{4,2},{5,3},{2,4},{3,5},{12,10},{13,11},{10,12},{11,13},{20,18},{2... | collective-permute-start | bytes 3145736 | tf_op jit(solution)/shard_map/second/ppermute | solution.py:636
  69.7 3.5 %open_up.1 = (bf16[384,768]{1,0:T(8,128)(2,1)S(1)}, bf16[384,768]{1,0:T(8,128)(2,1)S(1)}, bf16[384,768]{1,0:T(8,128)(2,1)S(1)}, bf16[384,768]{1,0:T(8,128)(2,1)S...) custom-call(s32[4]{0:T(128)S(1)} %pad_add_fusion.place_ref, f32[1,768]{1,0:T(1,128)S(1)} %copy-done.42, ...), custom_call_target="tpu_custom_call" | custom-call | flops 2415919104 | bytes 4194304 | tf_op jit(solution)/shard_map/open_up/pallas_call | solution.py:114
  74.4 3.5 collective-permute-done.9.refs_0_
  77.8 5.1 %collective-permute-start.16 = (bf16[384,1024]{1,0:T(8,128)(2,1)S(1)}, bf16[384,1024]{1,0:T(8,128)(2,1)S(1)}, u32[]{:S(2)}, u32[]{:S(2)}) collective-permute-start(bf16[384,1024]{1,0:T(8,128)(2,1)S(1)} %copy-done.61), channel_id=1, source_target_pairs={{4,2},{5,3},{2,4},{3,5},{12,10},{13,11},{10,12},{11,13},{20,18},{2... | collective-permute-start | bytes 2359304 | tf_op jit(solution)/shard_map/cotangent/ppermute | solution.py:636
  83.0 11.2 %attend.1 = (bf16[256,1536]{1,0:T(8,128)(2,1)S(1)}, f32[8,1536]{1,0:T(8,128)S(1)}, bf16[384,256]{1,0:T(8,128)(2,1)S(1)}, bf16[384,256]{1,0:T(8,128)(2,1)S(1)}, b...) custom-call(s32[4]{0:T(128)S(1)} %pad_add_fusion.place_ref, bf16[384,768]{1,0:T(8,128)(2,1)S(1)} %get-tuple-element.136.refs_0_, ...), custom_call_target="tpu_custom_call" | custom-call | flops 9663676416 | bytes 3145728 | tf_op jit(solution)/shard_map/attend/pallas_call | solution.py:190
  94.2 3.1 collective-permute-done.10.refs_5_.refs_1_
  98.0 1.6 collective-permute-start.14
  99.6 4.0 %collective-permute-done.12.refs_1_ = bf16[384,256]{1,0:T(8,128)(2,1)S(1)} collective-permute-done((bf16[384,256]{1,0:T(8,128)(2,1)S(1)}, bf16[384,256]{1,0:T(8,128)(2,1)S(1)}, u32[]{:S(2)}, u32[]{:S(2)}) %collective-permute-start.12) | collective-permute-done | bytes 196640 | tf_op jit(solution)/shard_map/ppermute | solution.py:638
  103.6 3.3 collective-permute-start.18
  106.9 3.1 collective-permute-start.19
  110.1 2.1 collective-permute-start.20
  115.6 4.0 %collective-permute-done.18.refs_1_ = bf16[512,1024]{1,0:T(8,128)(2,1)S(1)} collective-permute-done((bf16[512,1024]{1,0:T(8,128)(2,1)}, bf16[512,1024]{1,0:T(8,128)(2,1)S(1)}, u32[]{:S(2)}, u32[]{:S(2)}) %collective-permute-start.18) | collective-permute-done | bytes 1048608 | tf_op jit(solution)/shard_map/seconds/ppermute | solution.py:647
  119.9 14.2 %collective-permute-done.19.refs_2_ = bf16[512,1024]{1,0:T(8,128)(2,1)S(1)} collective-permute-done((bf16[512,1024]{1,0:T(8,128)(2,1)}, bf16[512,1024]{1,0:T(8,128)(2,1)S(1)}, u32[]{:S(2)}, u32[]{:S(2)}) %collective-permute-start.19) | collective-permute-done | bytes 1048608 | tf_op jit(solution)/shard_map/seconds/ppermute | solution.py:647
  134.2 9.9 %feed.2 = (bf16[768,1024]{1,0:T(8,128)(2,1)S(1)}, bf16[768,1024]{1,0:T(8,128)(2,1)S(1)}, f32[1,1024]{1,0:T(1,128)S(1)}, f32[384,1024]{1,0:T(8,128)S(1)}, f32[384...) custom-call(s32[4]{0:T(128)S(1)} %pad_add_fusion.place_ref, bf16[384,1024]{1,0:T(8,128)(2,1)S(1)} %get-tuple-element.173.x_one.refs_0_, ...), custom_call_target="tpu_custom_call" | custom-call | flops 6442450944 | bytes 4194304 | tf_op jit(solution)/shard_map/feed/pallas_call | solution.py:385
  147.7 4.6 %collective-permute-done.22.x_one.refs_2_ = bf16[384,1024]{1,0:T(8,128)(2,1)S(1)} collective-permute-done((bf16[384,1024]{1,0:T(8,128)(2,1)S(1)}, bf16[384,1024]{1,0:T(8,128)(2,1)S(1)}, u32[]{:S(2)}, u32[]{:S(2)}) %collective-permute-start.22) | collective-permute-done | bytes 786464 | tf_op jit(solution)/shard_map/secnear/ppermute | solution.py:638
  152.8 1.8 collective-permute-done.24.x_two.refs_3_
  155.7 8.8 %feed.3 = (bf16[768,1024]{1,0:T(8,128)(2,1)S(1)}, bf16[768,1024]{1,0:T(8,128)(2,1)S(1)}, f32[1,1024]{1,0:T(1,128)S(1)}, bf16[384,1024]{1,0:T(8,128)(2,1)S(1)}, b...) custom-call(s32[4]{0:T(128)S(1)} %pad_add_fusion.place_ref, ...), custom_call_target="tpu_custom_call" | custom-call | flops 6442450944 | bytes 4194304 | tf_op jit(solution)/shard_map/feed/pallas_call | solution.py:385
  165.7 3.0 collective-permute-done.26
  168.7 1.9 add_convert_fusion.4
  172.5 22.9 %weigh.1 = (bf16[2,256,1024]{2,1,0:T(8,128)(2,1)S(1)}, bf16[2,256,1024]{2,1,0:T(8,128)(2,1)}, bf16[2,256,1024]{2,1,0:T(8,128)(2,1)S(1)}, bf16[2,256,1024]{2,1,0:T(8,128)(2,1)}) custom-call(s32[4]{0:T(128)S(1)} %pad_add_fusion.place_ref, bf16[384,1024]{1,0:T(8,128)(2,1)S(1)} %get-tuple-element.173.x_one.refs_0_, ...), custom_call_target="tpu_custom_call" | custom-call | flops 6442450944 | bytes 16777216 | tf_op jit(solution)/shard_map/weigh/pallas_call | solution.py:454
  203.4 6.8 %unproject.1 = (bf16[384,1024]{1,0:T(8,128)(2,1)}, f32[384,1024]{1,0:T(8,128)}, f32[8,1024]{1,0:T(8,128)}, bf16[384,256]{1,0:T(8,128)(2,1)}, bf16[384,256]{1,0:T...) custom-call(f32[384,1024]{1,0:T(8,128)} %copy-done.9, ...), custom_call_target="tpu_custom_call" | custom-call | flops 805306368 | bytes 9175040 | tf_op jit(solution)/shard_map/unproject/pallas_call | solution.py:420
  211.6 1.6 collective-permute-start.31
  213.9 1.8 collective-permute-done.29.refs_5_
  215.7 6.0 %collective-permute-done.31.refs_7_ = bf16[384,256]{1,0:T(8,128)(2,1)S(1)} collective-permute-done((bf16[384,256]{1,0:T(8,128)(2,1)}, bf16[384,256]{1,0:T(8,128)(2,1)S(1)}, u32[]{:S(2)}, u32[]{:S(2)}) %collective-permute-start.31) | collective-permute-done | bytes 196640 | tf_op jit(solution)/shard_map/ppermute | solution.py:639
  221.7 2.0 add_convert_fusion.3
  223.8 1.9 add_convert_fusion
  226.1 1.9 add_convert_fusion.1
  228.4 7.5 %collective-permute-start.39 = (bf16[384,1024]{1,0:T(8,128)(2,1)S(1)}, bf16[384,1024]{1,0:T(8,128)(2,1)S(1)}, u32[]{:S(2)}, u32[]{:S(2)}) collective-permute-start(bf16[384,1024]{1,0:T(8,128)(2,1)S(1)} %add_convert_fusion.3), channel_id=1, source_target_pairs={{4,2},{5,3},{2,4},{3,5},{12,10},{13,11},{10,12},{11,13},{20,18},{2... | collective-permute-start | bytes 2359304 | tf_op jit(solution)/shard_map/output/ppermute | solution.py:636
  235.9 17.4 %attend_back.1.projected_ref = bf16[1536,768]{1,0:T(8,128)(2,1)S(1)} custom-call(s32[4]{0:T(128)S(1)} %pad_add_fusion.place_ref, bf16[384,768]{1,0:T(8,128)(2,1)S(1)} %copy-done.48, bf16[384,768]{1,0:T(8,128)(2,1)S(1)} %copy-done.50, bf16[384,768]{1,0:T(8,128)(2,1)S(1)} %copy-done.52, bf16[384,768]{1,0:T(8,128)(2,1)S(1)} %copy-done.54, ...), custom_call_target="tpu_custom_call" | custom-call | flops 24159191040 | bytes 7864320 | tf_op jit(solution)/shard_map/attend_back/pallas_call | solution.py:300
  255.9 2.6 share.1
  259.5 4.8 %weigh_late.1 = (bf16[2,256,512]{2,1,0:T(8,128)(2,1)S(1)}, bf16[2,256,512]{2,1,0:T(8,128)(2,1)S(1)}, bf16[2,256,512]{2,1,0:T(8,128)(2,1)S(1)}, bf16[2,256,512]{2...) custom-call(s32[4]{0:T(128)S(1)} %pad_add_fusion.place_ref, ...), custom_call_target="tpu_custom_call" | custom-call | flops 3221225472 | bytes 9437184 | tf_op jit(solution)/shard_map/weigh_late/pallas_call | solution.py:515
  270.1 2.3 convert_add_fusion
  274.2 6.1 %collective-permute-start.42 = (bf16[128,2048]{1,0:T(8,128)(2,1)S(1)}, bf16[128,2048]{1,0:T(8,128)(2,1)S(1)}, u32[]{:S(2)}, u32[]{:S(2)}) collective-permute-start(bf16[128,2048]{1,0:T(8,128)(2,1)S(1)} %get-tuple-element.281), channel_id=1, source_target_pairs={{4,2},{5,3},{2,4},{3,5},{12,10},{13,11},{10,12},{11,13},{20,18},{2... | collective-permute-start | bytes 1572872 | tf_op jit(solution)/shard_map/hand/ppermute | solution.py:636
  282.3 13.5 %collective-permute-done.42 = bf16[128,2048]{1,0:T(8,128)(2,1)S(1)} collective-permute-done((bf16[128,2048]{1,0:T(8,128)(2,1)S(1)}, bf16[128,2048]{1,0:T(8,128)(2,1)S(1)}, u32[]{:S(2)}, u32[]{:S(2)}) %collective-permute-start.42) | collective-permute-done | bytes 524320 | tf_op jit(solution)/shard_map/hand/ppermute | solution.py:636
  295.8 5.6 %collective-permute-done.43 = bf16[128,2048]{1,0:T(8,128)(2,1)S(1)} collective-permute-done((bf16[128,2048]{1,0:T(8,128)(2,1)S(1)}, bf16[128,2048]{1,0:T(8,128)(2,1)S(1)}, u32[]{:S(2)}, u32[]{:S(2)}) %collective-permute-start.43) | collective-permute-done | bytes 524320 | tf_op jit(solution)/shard_map/hand/ppermute | solution.py:742
  309.2 2.3 collective-permute-start.54
  313.6 7.2 %collective-permute-start.55 = (bf16[128,1024]{1,0:T(8,128)(2,1)S(1)}, bf16[128,1024]{1,0:T(8,128)(2,1)S(1)}, u32[]{:S(2)}, u32[]{:S(2)}) collective-permute-start(bf16[128,1024]{1,0:T(8,128)(2,1)S(1)} %get-tuple-element.282), channel_id=1, source_target_pairs={{4,2},{5,3},{2,4},{3,5},{12,10},{13,11},{10,12},{11,13},{20,18},{2... | collective-permute-start | bytes 786440 | tf_op jit(solution)/shard_map/latehand/ppermute | solution.py:636
  320.9 1.9 collective-permute-start.52
  324.7 14.2 %collective-permute-done.55 = bf16[128,1024]{1,0:T(8,128)(2,1)S(1)} collective-permute-done((bf16[128,1024]{1,0:T(8,128)(2,1)S(1)}, bf16[128,1024]{1,0:T(8,128)(2,1)S(1)}, u32[]{:S(2)}, u32[]{:S(2)}) %collective-permute-start.55) | collective-permute-done | bytes 262176 | tf_op jit(solution)/shard_map/latehand/ppermute | solution.py:636
  341.0 9.2 %collective-permute-done.52 = bf16[384,1024]{1,0:T(8,128)(2,1)S(1)} collective-permute-done((bf16[384,1024]{1,0:T(8,128)(2,1)S(1)}, bf16[384,1024]{1,0:T(8,128)(2,1)S(1)}, u32[]{:S(2)}, u32[]{:S(2)}) %collective-permute-start.52) | collective-permute-done | bytes 786464 | tf_op jit(solution)/shard_map/ppermute | solution.py:636
  (297 shorter events, 75.3 us)
Async XLA Ops:
  0.6 28.1 %collective-permute-start = (bf16[384,1024]{1,0:T(8,128)(2,1)}, bf16[384,1024]{1,0:T(8,128)(2,1)S(1)}, u32[]{:S(2)}, u32[]{:S(2)}) collective-permute-start(bf16[384,1024]{1,0:T(8,128)(2,1)} %param.15), channel_id=1, source_target_pairs={{4,2},{5,3},{2,4},{3,5},{12,10},{13,11},{10,12},{11,13},{20,18},{2... | collective-permute-start | bytes 2359304 | tf_op jit(solution)/shard_map/ppermute | solution.py:636
  8.3 20.5 %collective-permute-start.1 = (f32[16,128]{1,0:T(8,128)S(1)}, f32[16,128]{1,0:T(8,128)S(1)}, u32[]{:S(2)}, u32[]{:S(2)}) collective-permute-start(f32[16,128]{1,0:T(8,128)S(1)} %fusion.20), channel_id=1, source_target_pairs={{4,2},{5,3},{2,4},{3,5},{12,10},{13,11},{10,12},{11,13},{20,18},{2... | collective-permute-start | bytes 24584 | tf_op jit(solution)/shard_map/notes/ppermute | solution.py:636
  12.7 23.2 %collective-permute-start.2 = (bf16[256,1024]{1,0:T(8,128)(2,1)S(1)}, bf16[256,1024]{1,0:T(8,128)(2,1)S(1)}, u32[]{:S(2)}, u32[]{:S(2)}) collective-permute-start(bf16[256,1024]{1,0:T(8,128)(2,1)S(1)} %pad_maximum_fusion.2), channel_id=1, source_target_pairs={{4,2},{5,3},{2,4},{3,5},{12,10},{13,11},{10,12},{11,13},{20,18},{2... | collective-permute-start | bytes 1572872 | tf_op jit(solution)/shard_map/first/ppermute | solution.py:636
  36.0 20.7 %collective-permute-start.3 = (bf16[384,1024]{1,0:T(8,128)(2,1)S(1)}, bf16[384,1024]{1,0:T(8,128)(2,1)S(1)}, u32[]{:S(2)}, u32[]{:S(2)}) collective-permute-start(bf16[384,1024]{1,0:T(8,128)(2,1)S(1)} %fusion.6.refs_4_.refs_0_), channel_id=1, source_target_pairs={{0,1},{1,0},{2,3},{3,2},{4,5},{5,4},{6,7},{7,6},{8,9},{9,8},{10,11... | collective-permute-start | bytes 2359304 | tf_op jit(solution)/shard_map/ppermute | solution.py:638
  36.4 20.3 %collective-permute-start.4 = (bf16[384,1024]{1,0:T(8,128)(2,1)S(1)}, bf16[384,1024]{1,0:T(8,128)(2,1)S(1)}, u32[]{:S(2)}, u32[]{:S(2)}) collective-permute-start(bf16[384,1024]{1,0:T(8,128)(2,1)S(1)} %fusion.6.refs_4_.refs_0_), channel_id=1, source_target_pairs={{0,4},{4,0},{8,12},{12,8},{16,20},{20,16},{24,28},{28,24},{1,5},{5... | collective-permute-start | bytes 2359304 | tf_op jit(solution)/shard_map/ppermute | solution.py:637
  36.4 10.7 %collective-permute-start.5 = (bf16[256,1024]{1,0:T(8,128)(2,1)S(1)}, bf16[256,1024]{1,0:T(8,128)(2,1)S(1)}, u32[]{:S(2)}, u32[]{:S(2)}) collective-permute-start(bf16[256,1024]{1,0:T(8,128)(2,1)S(1)} %collective-permute-done.2.refs_0_), channel_id=1, source_target_pairs={{4,12},{5,13},{2,10},{3,11},{12,4},{13,5},{10,2},{11,3},{20,28},{2... | collective-permute-start | bytes 1572872 | tf_op jit(solution)/shard_map/pieces/ppermute | solution.py:647
  39.5 15.5 %collective-permute-start.6 = (bf16[256,1024]{1,0:T(8,128)(2,1)S(1)}, bf16[256,1024]{1,0:T(8,128)(2,1)S(1)}, u32[]{:S(2)}, u32[]{:S(2)}) collective-permute-start(bf16[256,1024]{1,0:T(8,128)(2,1)S(1)} %collective-permute-done.2.refs_0_), channel_id=1, source_target_pairs={{4,20},{5,21},{2,18},{3,19},{12,28},{13,29},{10,26},{11,27},{20,4}... | collective-permute-start | bytes 1572872 | tf_op jit(solution)/shard_map/pieces/ppermute | solution.py:647
  42.7 13.2 %collective-permute-start.7 = (bf16[256,1024]{1,0:T(8,128)(2,1)S(1)}, bf16[256,1024]{1,0:T(8,128)(2,1)S(1)}, u32[]{:S(2)}, u32[]{:S(2)}) collective-permute-start(bf16[256,1024]{1,0:T(8,128)(2,1)S(1)} %collective-permute-done.2.refs_0_), channel_id=1, source_target_pairs={{4,28},{5,29},{2,26},{3,27},{12,20},{13,21},{10,18},{11,19},{20,12... | collective-permute-start | bytes 1572872 | tf_op jit(solution)/shard_map/pieces/ppermute | solution.py:647
  47.9 29.9 %collective-permute-start.9 = (bf16[512,1024]{1,0:T(8,128)(2,1)}, bf16[512,1024]{1,0:T(8,128)(2,1)}, u32[]{:S(2)}, u32[]{:S(2)}) collective-permute-start(bf16[512,1024]{1,0:T(8,128)(2,1)} %pad_maximum_fusion), channel_id=1, source_target_pairs={{4,2},{5,3},{2,4},{3,5},{12,10},{13,11},{10,12},{11,13},{20,18},{2... | collective-permute-start | bytes 3145736 | tf_op jit(solution)/shard_map/second/ppermute | solution.py:636
  77.8 19.5 %collective-permute-start.10 = (bf16[1024,256]{1,0:T(8,128)(2,1)S(1)}, bf16[1024,256]{1,0:T(8,128)(2,1)S(1)}, u32[]{:S(2)}, u32[]{:S(2)}) collective-permute-start(bf16[1024,256]{1,0:T(8,128)(2,1)S(1)} %get-tuple-element.146.refs_4_.refs_0_), channel_id=1, source_target_pairs={{0,1},{1,0},{2,3},{3,2},{4,5},{5,4},{6,7},{7,6},{8,9},{9,8},{10,11... | collective-permute-start | bytes 1572872 | tf_op jit(solution)/shard_map/outs/ppermute | solution.py:638
  77.8 19.5 %collective-permute-start.11 = (bf16[1024,256]{1,0:T(8,128)(2,1)S(1)}, bf16[1024,256]{1,0:T(8,128)(2,1)S(1)}, u32[]{:S(2)}, u32[]{:S(2)}) collective-permute-start(bf16[1024,256]{1,0:T(8,128)(2,1)S(1)} %get-tuple-element.146.refs_4_.refs_0_), channel_id=1, source_target_pairs={{0,4},{4,0},{8,12},{12,8},{16,20},{20,16},{24,28},{28,24},{1,5},{5... | collective-permute-start | bytes 1572872 | tf_op jit(solution)/shard_map/outs/ppermute | solution.py:637
  77.8 37.1 %collective-permute-start.16 = (bf16[384,1024]{1,0:T(8,128)(2,1)S(1)}, bf16[384,1024]{1,0:T(8,128)(2,1)S(1)}, u32[]{:S(2)}, u32[]{:S(2)}) collective-permute-start(bf16[384,1024]{1,0:T(8,128)(2,1)S(1)} %copy-done.61), channel_id=1, source_target_pairs={{4,2},{5,3},{2,4},{3,5},{12,10},{13,11},{10,12},{11,13},{20,18},{2... | collective-permute-start | bytes 2359304 | tf_op jit(solution)/shard_map/cotangent/ppermute | solution.py:636
  97.4 14.8 %collective-permute-start.15 = (bf16[1024,256]{1,0:T(8,128)(2,1)S(1)}, bf16[1024,256]{1,0:T(8,128)(2,1)S(1)}, u32[]{:S(2)}, u32[]{:S(2)}) collective-permute-start(bf16[1024,256]{1,0:T(8,128)(2,1)S(1)} %collective-permute-done.10.refs_5_.refs_1_), channel_id=1, source_target_pairs={{0,4},{4,0},{8,12},{12,8},{16,20},{20,16},{24,28},{28,24},{1,5},{5... | collective-permute-start | bytes 1572872 | tf_op jit(solution)/shard_map/last/ppermute | solution.py:637
  97.4 6.1 %collective-permute-start.12 = (bf16[384,256]{1,0:T(8,128)(2,1)S(1)}, bf16[384,256]{1,0:T(8,128)(2,1)S(1)}, u32[]{:S(2)}, u32[]{:S(2)}) collective-permute-start(bf16[384,256]{1,0:T(8,128)(2,1)S(1)} %get-tuple-element.147), channel_id=1, source_target_pairs={{0,1},{1,0},{2,3},{3,2},{4,5},{5,4},{6,7},{7,6},{8,9},{9,8},{10,11... | collective-permute-start | bytes 589832 | tf_op jit(solution)/shard_map/ppermute | solution.py:638
  97.5 9.4 %collective-permute-start.13 = (bf16[384,256]{1,0:T(8,128)(2,1)S(1)}, bf16[384,256]{1,0:T(8,128)(2,1)S(1)}, u32[]{:S(2)}, u32[]{:S(2)}) collective-permute-start(bf16[384,256]{1,0:T(8,128)(2,1)S(1)} %get-tuple-element.148), channel_id=1, source_target_pairs={{0,4},{4,0},{8,12},{12,8},{16,20},{20,16},{24,28},{28,24},{1,5},{5... | collective-permute-start | bytes 589832 | tf_op jit(solution)/shard_map/ppermute | solution.py:637
  98.0 12.1 %collective-permute-start.14 = (bf16[384,256]{1,0:T(8,128)(2,1)S(1)}, bf16[384,256]{1,0:T(8,128)(2,1)S(1)}, u32[]{:S(2)}, u32[]{:S(2)}) collective-permute-start(bf16[384,256]{1,0:T(8,128)(2,1)S(1)} %get-tuple-element.149), channel_id=1, source_target_pairs={{0,5},{1,4},{2,7},{3,6},{4,1},{5,0},{6,3},{7,2},{8,13},{9,12},{10,... | collective-permute-start | bytes 589832 | tf_op jit(solution)/shard_map/ppermute | solution.py:639
  103.6 16.0 %collective-permute-start.18 = (bf16[512,1024]{1,0:T(8,128)(2,1)}, bf16[512,1024]{1,0:T(8,128)(2,1)S(1)}, u32[]{:S(2)}, u32[]{:S(2)}) collective-permute-start(bf16[512,1024]{1,0:T(8,128)(2,1)} %collective-permute-done.9.refs_0_), channel_id=1, source_target_pairs={{4,12},{5,13},{2,10},{3,11},{12,4},{13,5},{10,2},{11,3},{20,28},{2... | collective-permute-start | bytes 3145736 | tf_op jit(solution)/shard_map/seconds/ppermute | solution.py:647
  106.9 27.3 %collective-permute-start.19 = (bf16[512,1024]{1,0:T(8,128)(2,1)}, bf16[512,1024]{1,0:T(8,128)(2,1)S(1)}, u32[]{:S(2)}, u32[]{:S(2)}) collective-permute-start(bf16[512,1024]{1,0:T(8,128)(2,1)} %collective-permute-done.9.refs_0_), channel_id=1, source_target_pairs={{4,20},{5,21},{2,18},{3,19},{12,28},{13,29},{10,26},{11,27},{20,4}... | collective-permute-start | bytes 3145736 | tf_op jit(solution)/shard_map/seconds/ppermute | solution.py:647
  110.1 24.1 %collective-permute-start.20 = (bf16[512,1024]{1,0:T(8,128)(2,1)}, bf16[512,1024]{1,0:T(8,128)(2,1)S(1)}, u32[]{:S(2)}, u32[]{:S(2)}) collective-permute-start(bf16[512,1024]{1,0:T(8,128)(2,1)} %collective-permute-done.9.refs_0_), channel_id=1, source_target_pairs={{4,28},{5,29},{2,26},{3,27},{12,20},{13,21},{10,18},{11,19},{20,12... | collective-permute-start | bytes 3145736 | tf_op jit(solution)/shard_map/seconds/ppermute | solution.py:647
  115.0 19.2 %collective-permute-start.17 = (bf16[384,1024]{1,0:T(8,128)(2,1)S(1)}, bf16[384,1024]{1,0:T(8,128)(2,1)S(1)}, u32[]{:S(2)}, u32[]{:S(2)}) collective-permute-start(bf16[384,1024]{1,0:T(8,128)(2,1)S(1)} %get-tuple-element.173.x_one.refs_0_), channel_id=1, source_target_pairs={{0,4},{4,0},{8,12},{12,8},{16,20},{20,16},{24,28},{28,24},{1,5},{5... | collective-permute-start | bytes 2359304 | tf_op jit(solution)/shard_map/ppermute | solution.py:637
  115.1 19.1 %collective-permute-start.21 = (bf16[384,1024]{1,0:T(8,128)(2,1)S(1)}, bf16[384,1024]{1,0:T(8,128)(2,1)S(1)}, u32[]{:S(2)}, u32[]{:S(2)}) collective-permute-start(bf16[384,1024]{1,0:T(8,128)(2,1)S(1)} %broadcast_select_fusion.2.g_one.refs_4_.cotangent_ref), channel_id=1, source_target_pairs={{0,4},{4,0},{8,12},{12,8},{16,20},{20,16},{24,28},{28,24},{1,5},{5... | collective-permute-start | bytes 2359304 | tf_op jit(solution)/shard_map/ppermute | solution.py:637
  119.6 28.1 %collective-permute-start.23 = (bf16[384,1024]{1,0:T(8,128)(2,1)S(1)}, bf16[384,1024]{1,0:T(8,128)(2,1)S(1)}, u32[]{:S(2)}, u32[]{:S(2)}) collective-permute-start(bf16[384,1024]{1,0:T(8,128)(2,1)S(1)} %broadcast_select_fusion.2.g_one.refs_4_.cotangent_ref), channel_id=1, source_target_pairs={{0,1},{1,0},{2,3},{3,2},{4,5},{5,4},{6,7},{7,6},{8,9},{9,8},{10,11... | collective-permute-start | bytes 2359304 | tf_op jit(solution)/shard_map/cotnear/ppermute | solution.py:638
  134.2 18.1 %collective-permute-start.22 = (bf16[384,1024]{1,0:T(8,128)(2,1)S(1)}, bf16[384,1024]{1,0:T(8,128)(2,1)S(1)}, u32[]{:S(2)}, u32[]{:S(2)}) collective-permute-start(bf16[384,1024]{1,0:T(8,128)(2,1)S(1)} %get-tuple-element.173.x_one.refs_0_), channel_id=1, source_target_pairs={{0,1},{1,0},{2,3},{3,2},{4,5},{5,4},{6,7},{7,6},{8,9},{9,8},{10,11... | collective-permute-start | bytes 2359304 | tf_op jit(solution)/shard_map/secnear/ppermute | solution.py:638
  170.6 32.8 %collective-permute-start.28 = (bf16[768,1024]{1,0:T(8,128)(2,1)}, bf16[768,1024]{1,0:T(8,128)(2,1)}, u32[]{:S(2)}, u32[]{:S(2)}) collective-permute-start(bf16[768,1024]{1,0:T(8,128)(2,1)} %get-tuple-element.179), channel_id=1, source_target_pairs={{0,4},{4,0},{8,12},{12,8},{16,20},{20,16},{24,28},{28,24},{1,5},{5... | collective-permute-start | bytes 4718600 | tf_op jit(solution)/shard_map/two/ppermute | solution.py:637
  171.0 32.4 %collective-permute-start.27 = (bf16[384,1024]{1,0:T(8,128)(2,1)}, bf16[384,1024]{1,0:T(8,128)(2,1)}, u32[]{:S(2)}, u32[]{:S(2)}) collective-permute-start(bf16[384,1024]{1,0:T(8,128)(2,1)} %get-tuple-element.277), channel_id=1, source_target_pairs={{0,1},{1,0},{2,3},{3,2},{4,5},{5,4},{6,7},{7,6},{8,9},{9,8},{10,11... | collective-permute-start | bytes 2359304 | tf_op jit(solution)/shard_map/ppermute | solution.py:638
  171.1 40.5 %collective-permute-start.32 = (bf16[384,1024]{1,0:T(8,128)(2,1)}, bf16[384,1024]{1,0:T(8,128)(2,1)}, u32[]{:S(2)}, u32[]{:S(2)}) collective-permute-start(bf16[384,1024]{1,0:T(8,128)(2,1)} %get-tuple-element.276), channel_id=1, source_target_pairs={{0,1},{1,0},{2,3},{3,2},{4,5},{5,4},{6,7},{7,6},{8,9},{9,8},{10,11... | collective-permute-start | bytes 2359304 | tf_op jit(solution)/shard_map/out/ppermute | solution.py:638
  196.4 27.4 %collective-permute-start.33 = (bf16[2,256,1024]{2,1,0:T(8,128)(2,1)}, bf16[2,256,1024]{2,1,0:T(8,128)(2,1)}, u32[]{:S(2)}, u32[]{:S(2)}) collective-permute-start(bf16[2,256,1024]{2,1,0:T(8,128)(2,1)} %get-tuple-element.191), channel_id=1, source_target_pairs={{0,8},{4,12},{8,0},{12,4},{16,24},{20,28},{24,16},{28,20},{1,9},{5... | collective-permute-start | bytes 3145736 | tf_op jit(solution)/shard_map/fed/ppermute | solution.py:640
  197.6 26.2 %collective-permute-start.34 = (bf16[2,256,1024]{2,1,0:T(8,128)(2,1)}, bf16[2,256,1024]{2,1,0:T(8,128)(2,1)}, u32[]{:S(2)}, u32[]{:S(2)}) collective-permute-start(bf16[2,256,1024]{2,1,0:T(8,128)(2,1)} %get-tuple-element.192), channel_id=1, source_target_pairs={{0,16},{4,20},{8,24},{12,28},{16,0},{20,4},{24,8},{28,12},{1,17},{... | collective-permute-start | bytes 3145736 | tf_op jit(solution)/shard_map/fed/ppermute | solution.py:640
  210.2 5.4 %collective-permute-start.29 = (bf16[384,256]{1,0:T(8,128)(2,1)}, bf16[384,256]{1,0:T(8,128)(2,1)S(1)}, u32[]{:S(2)}, u32[]{:S(2)}) collective-permute-start(bf16[384,256]{1,0:T(8,128)(2,1)} %get-tuple-element.183), channel_id=1, source_target_pairs={{0,1},{1,0},{2,3},{3,2},{4,5},{5,4},{6,7},{7,6},{8,9},{9,8},{10,11... | collective-permute-start | bytes 589832 | tf_op jit(solution)/shard_map/ppermute | solution.py:638
  211.6 10.1 %collective-permute-start.31 = (bf16[384,256]{1,0:T(8,128)(2,1)}, bf16[384,256]{1,0:T(8,128)(2,1)S(1)}, u32[]{:S(2)}, u32[]{:S(2)}) collective-permute-start(bf16[384,256]{1,0:T(8,128)(2,1)} %get-tuple-element.185), channel_id=1, source_target_pairs={{0,5},{1,4},{2,7},{3,6},{4,1},{5,0},{6,3},{7,2},{8,13},{9,12},{10,... | collective-permute-start | bytes 589832 | tf_op jit(solution)/shard_map/ppermute | solution.py:639
  221.7 32.3 %collective-permute-start.35 = (bf16[384,1024]{1,0:T(8,128)(2,1)}, bf16[384,1024]{1,0:T(8,128)(2,1)S(1)}, u32[]{:S(2)}, u32[]{:S(2)}) collective-permute-start(bf16[384,1024]{1,0:T(8,128)(2,1)} %get-tuple-element.202.refs_0_), channel_id=1, source_target_pairs={{0,4},{4,0},{8,12},{12,8},{16,20},{20,16},{24,28},{28,24},{1,5},{5... | collective-permute-start | bytes 2359304 | tf_op jit(solution)/shard_map/low/ppermute | solution.py:637
  221.7 32.3 %collective-permute-start.36 = (bf16[384,1024]{1,0:T(8,128)(2,1)}, bf16[384,1024]{1,0:T(8,128)(2,1)S(1)}, u32[]{:S(2)}, u32[]{:S(2)}) collective-permute-start(bf16[384,1024]{1,0:T(8,128)(2,1)} %get-tuple-element.202.refs_0_), channel_id=1, source_target_pairs={{0,1},{1,0},{2,3},{3,2},{4,5},{5,4},{6,7},{7,6},{8,9},{9,8},{10,11... | collective-permute-start | bytes 2359304 | tf_op jit(solution)/shard_map/low/ppermute | solution.py:638
  225.8 27.6 %collective-permute-start.38 = (bf16[1,256,1024]{2,1,0:T(8,128)(2,1)S(1)}, bf16[1,256,1024]{2,1,0:T(8,128)(2,1)S(1)}, u32[]{:S(2)}, u32[]{:S(2)}) collective-permute-start(bf16[1,256,1024]{2,1,0:T(8,128)(2,1)S(1)} %slice.181), channel_id=1, source_target_pairs={{0,8},{4,12},{8,0},{12,4},{16,24},{20,28},{24,16},{28,20},{1,9},{5... | collective-permute-start | bytes 1572872 | tf_op jit(solution)/shard_map/fedrest/ppermute | solution.py:640
  228.1 25.3 %collective-permute-start.37 = (bf16[1,256,1024]{2,1,0:T(8,128)(2,1)S(1)}, bf16[1,256,1024]{2,1,0:T(8,128)(2,1)S(1)}, u32[]{:S(2)}, u32[]{:S(2)}) collective-permute-start(bf16[1,256,1024]{2,1,0:T(8,128)(2,1)S(1)} %slice.180), channel_id=1, source_target_pairs={{0,16},{4,20},{8,24},{12,28},{16,0},{20,4},{24,8},{28,12},{1,17},{... | collective-permute-start | bytes 1572872 | tf_op jit(solution)/shard_map/fedrest/ppermute | solution.py:640
  228.4 25.6 %collective-permute-start.39 = (bf16[384,1024]{1,0:T(8,128)(2,1)S(1)}, bf16[384,1024]{1,0:T(8,128)(2,1)S(1)}, u32[]{:S(2)}, u32[]{:S(2)}) collective-permute-start(bf16[384,1024]{1,0:T(8,128)(2,1)S(1)} %add_convert_fusion.3), channel_id=1, source_target_pairs={{4,2},{5,3},{2,4},{3,5},{12,10},{13,11},{10,12},{11,13},{20,18},{2... | collective-permute-start | bytes 2359304 | tf_op jit(solution)/shard_map/output/ppermute | solution.py:636
  254.0 5.5 %collective-permute-start.44 = (bf16[384,1024]{1,0:T(8,128)(2,1)S(1)}, bf16[384,1024]{1,0:T(8,128)(2,1)S(1)}, u32[]{:S(2)}, u32[]{:S(2)}) collective-permute-start(bf16[384,1024]{1,0:T(8,128)(2,1)S(1)} %collective-permute-done.36.refs_1_), channel_id=1, source_target_pairs={{0,4},{4,0},{8,12},{12,8},{16,20},{20,16},{24,28},{28,24},{1,5},{5... | collective-permute-start | bytes 2359304 | tf_op jit(solution)/shard_map/ppermute | solution.py:637
  258.6 11.6 %collective-permute-start.40 = (bf16[768,1024]{1,0:T(8,128)(2,1)}, bf16[768,1024]{1,0:T(8,128)(2,1)}, u32[]{:S(2)}, u32[]{:S(2)}) collective-permute-start(bf16[768,1024]{1,0:T(8,128)(2,1)} %get-tuple-element.215), channel_id=1, source_target_pairs={{0,4},{4,0},{8,12},{12,8},{16,20},{20,16},{24,28},{28,24},{1,5},{5... | collective-permute-start | bytes 4718600 | tf_op jit(solution)/shard_map/ppermute | solution.py:637
  272.4 29.7 %collective-permute-start.41 = (bf16[384,1024]{1,0:T(8,128)(2,1)S(1)}, bf16[384,1024]{1,0:T(8,128)(2,1)S(1)}, u32[]{:S(2)}, u32[]{:S(2)}) collective-permute-start(bf16[384,1024]{1,0:T(8,128)(2,1)S(1)} %get-tuple-element.275), channel_id=1, source_target_pairs={{0,1},{1,0},{2,3},{3,2},{4,5},{5,4},{6,7},{7,6},{8,9},{9,8},{10,11... | collective-permute-start | bytes 2359304 | tf_op jit(solution)/shard_map/ppermute | solution.py:638
  272.7 8.3 %collective-permute-start.49 = (f32[96,128]{1,0:T(8,128)S(1)}, f32[96,128]{1,0:T(8,128)S(1)}, u32[]{:S(2)}, u32[]{:S(2)}) collective-permute-start(f32[96,128]{1,0:T(8,128)S(1)} %fusion.22), channel_id=1, source_target_pairs={{0,16},{4,20},{8,24},{12,28},{16,0},{20,4},{24,8},{28,12},{1,17},{... | collective-permute-start | bytes 147464 | tf_op jit(solution)/shard_map/ppermute | solution.py:559
  274.2 21.6 %collective-permute-start.42 = (bf16[128,2048]{1,0:T(8,128)(2,1)S(1)}, bf16[128,2048]{1,0:T(8,128)(2,1)S(1)}, u32[]{:S(2)}, u32[]{:S(2)}) collective-permute-start(bf16[128,2048]{1,0:T(8,128)(2,1)S(1)} %get-tuple-element.281), channel_id=1, source_target_pairs={{4,2},{5,3},{2,4},{3,5},{12,10},{13,11},{10,12},{11,13},{20,18},{2... | collective-permute-start | bytes 1572872 | tf_op jit(solution)/shard_map/hand/ppermute | solution.py:636
  280.2 21.2 %collective-permute-start.43 = (bf16[128,2048]{1,0:T(8,128)(2,1)S(1)}, bf16[128,2048]{1,0:T(8,128)(2,1)S(1)}, u32[]{:S(2)}, u32[]{:S(2)}) collective-permute-start(bf16[128,2048]{1,0:T(8,128)(2,1)S(1)} %get-tuple-element.280), channel_id=1, source_target_pairs={{4,6},{5,7},{2,0},{3,1},{12,14},{13,15},{10,8},{11,9},{20,22},{21,... | collective-permute-start | bytes 1572872 | tf_op jit(solution)/shard_map/hand/ppermute | solution.py:742
  280.3 21.1 %collective-permute-start.45 = (bf16[2,256,512]{2,1,0:T(8,128)(2,1)S(1)}, bf16[2,256,512]{2,1,0:T(8,128)(2,1)S(1)}, u32[]{:S(2)}, u32[]{:S(2)}) collective-permute-start(bf16[2,256,512]{2,1,0:T(8,128)(2,1)S(1)} %copy-done.34), channel_id=1, source_target_pairs={{0,8},{4,12},{8,0},{12,4},{16,24},{20,28},{24,16},{28,20},{1,9},{5... | collective-permute-start | bytes 1572872 | tf_op jit(solution)/shard_map/late/ppermute | solution.py:640
  281.1 20.3 %collective-permute-start.46 = (bf16[2,256,512]{2,1,0:T(8,128)(2,1)S(1)}, bf16[2,256,512]{2,1,0:T(8,128)(2,1)S(1)}, u32[]{:S(2)}, u32[]{:S(2)}) collective-permute-start(bf16[2,256,512]{2,1,0:T(8,128)(2,1)S(1)} %copy-done.32), channel_id=1, source_target_pairs={{0,16},{4,20},{8,24},{12,28},{16,0},{20,4},{24,8},{28,12},{1,17},{... | collective-permute-start | bytes 1572872 | tf_op jit(solution)/shard_map/late/ppermute | solution.py:640
  303.0 10.4 %collective-permute-start.51 = (bf16[1,256,512]{2,1,0:T(8,128)(2,1)}, bf16[1,256,512]{2,1,0:T(8,128)(2,1)S(1)}, u32[]{:S(2)}, u32[]{:S(2)}) collective-permute-start(bf16[1,256,512]{2,1,0:T(8,128)(2,1)} %slice.187), channel_id=1, source_target_pairs={{0,8},{4,12},{8,0},{12,4},{16,24},{20,28},{24,16},{28,20},{1,9},{5... | collective-permute-start | bytes 786440 | tf_op jit(solution)/shard_map/laterest/ppermute | solution.py:640
  303.9 9.5 %collective-permute-start.50 = (bf16[1,256,512]{2,1,0:T(8,128)(2,1)S(1)}, bf16[1,256,512]{2,1,0:T(8,128)(2,1)S(1)}, u32[]{:S(2)}, u32[]{:S(2)}) collective-permute-start(bf16[1,256,512]{2,1,0:T(8,128)(2,1)S(1)} %slice.186), channel_id=1, source_target_pairs={{0,16},{4,20},{8,24},{12,28},{16,0},{20,4},{24,8},{28,12},{1,17},{... | collective-permute-start | bytes 786440 | tf_op jit(solution)/shard_map/laterest/ppermute | solution.py:640
  313.6 25.3 %collective-permute-start.55 = (bf16[128,1024]{1,0:T(8,128)(2,1)S(1)}, bf16[128,1024]{1,0:T(8,128)(2,1)S(1)}, u32[]{:S(2)}, u32[]{:S(2)}) collective-permute-start(bf16[128,1024]{1,0:T(8,128)(2,1)S(1)} %get-tuple-element.282), channel_id=1, source_target_pairs={{4,2},{5,3},{2,4},{3,5},{12,10},{13,11},{10,12},{11,13},{20,18},{2... | collective-permute-start | bytes 786440 | tf_op jit(solution)/shard_map/latehand/ppermute | solution.py:636
  320.9 18.1 %collective-permute-start.56 = (bf16[128,1024]{1,0:T(8,128)(2,1)S(1)}, bf16[128,1024]{1,0:T(8,128)(2,1)S(1)}, u32[]{:S(2)}, u32[]{:S(2)}) collective-permute-start(bf16[128,1024]{1,0:T(8,128)(2,1)S(1)} %get-tuple-element.283), channel_id=1, source_target_pairs={{4,6},{5,7},{2,0},{3,1},{12,14},{13,15},{10,8},{11,9},{20,22},{21,... | collective-permute-start | bytes 786440 | tf_op jit(solution)/shard_map/latehand/ppermute | solution.py:742
  320.9 29.2 %collective-permute-start.52 = (bf16[384,1024]{1,0:T(8,128)(2,1)S(1)}, bf16[384,1024]{1,0:T(8,128)(2,1)S(1)}, u32[]{:S(2)}, u32[]{:S(2)}) collective-permute-start(bf16[384,1024]{1,0:T(8,128)(2,1)S(1)} %fusion.11), channel_id=1, source_target_pairs={{4,2},{5,3},{2,4},{3,5},{12,10},{13,11},{10,12},{11,13},{20,18},{2... | collective-permute-start | bytes 2359304 | tf_op jit(solution)/shard_map/ppermute | solution.py:636
  (77 other events, 670.0 us)
where the time goes:
time: 358 us; the launch traced here: 351 us
  waiting for transfers between devices  113 us (32%)
  Pallas kernels  90.2 us (25%)
  starting transfers between devices  85.9 us (24%)
  local copies, waits for them, and re-layouts  40.9 us (11%)
  other arithmetic  18.4 us (5%)
    ppermute x9, waiting for transfers between devices, body(): far = lambda value: lax.ppermute(value, both, far_pairs)  58.6 us
    ppermute x9, starting transfers between devices, body(): far = lambda value: lax.ppermute(value, both, far_pairs)  46.2 us
    unnamed x147, local copies, waits for them, and re-layouts  31.8 us
    pallas_call x1, Pallas kernels, weigh(): pl.pallas_call(weigh_kernel, in_specs=[in_smem()] + [in_vmem()] * (2 * le...  22.9 us
    ppermute x6, waiting for transfers between devices, spread(): lax.ppermute(value, both, away_pairs(block))  19 us
    pallas_call x2, Pallas kernels, feed(): pl.pallas_call(functools.partial(feed_kernel, len(pieces)), in_specs=[in_...  18.7 us
    pallas_call x1, Pallas kernels, attend_back(): pl.pallas_call(attend_back_kernel, out_shape=shaped((rows, 3 * width), LO...  17.4 us
    ppermute x6, starting transfers between devices, spread(): lax.ppermute(value, both, away_pairs(block))  16.9 us
  transfers between devices with their start and end apart: 57, of which 23 were waited for; matrix products, arithmetic and copies ran while one was open for 8% of the time, Pallas kernels for 23%

commit v1 on v0

--- a/solution.py
+++ b/solution.py
@@ -422,7 +422,7 @@
         out_shape=[shaped((rows, width), LOW), shaped((rows, width), WIDE), shaped((8, width), WIDE)] + [shaped((rows, part), LOW)] * members,
         in_specs=[in_vmem()] * (6 + members),
         out_specs=[in_vmem()] * (3 + members),
-        compiler_params=params(56),
+        compiler_params=params(24),
         cost_estimate=pl.CostEstimate(flops=2 * rows * width * width, bytes_accessed=2 * width * width + 18 * rows * width, transcendentals=rows),
         name="unproject",
     )(own, mate, near, middle, cotangent, gain, *outs)
@@ -565,7 +565,7 @@
         bit *= 2
     return values
 
-PLAN = {'first': (None, 1), 'notes': (None, 0), 'cotangent': (3, 6), 'second': (None, 3), 'pieces': (None, 2), 'outs': (None, 4), 'seconds': (None, 70), 'last': (None, 5), 'cotmate': (None, 7), 'cotnear': (None, 8), 'secnear': (None, 8), 'two': (11, 12), 'three': (11, None), 'fed': (None, 15), 'out': (None, 14), 'low': (None, 16), 'fedrest': (None, 16), 'hand': (None, 20), 'output': (None, 16), 'late': (None, 20), 'laterest': (None, 21), 'latehand': (None, None), 'early': 1, 'half': 1, 'sums': 19, 'middle': 20, 'wide': 0, 'lateend': 1}
+PLAN = {'first': (None, 1), 'notes': (None, 0), 'cotangent': (3, 6), 'second': (None, 3), 'pieces': (None, 2), 'outs': (None, 4), 'seconds': (None, 70), 'last': (None, 5), 'cotmate': (None, 7), 'cotnear': (None, 8), 'secnear': (None, 8), 'two': (11, 12), 'three': (11, None), 'fed': (None, 15), 'out': (None, 14), 'low': (None, 16), 'fedrest': (None, 16), 'hand': (None, None), 'output': (None, 16), 'late': (None, 20), 'laterest': (None, 21), 'latehand': (None, None), 'early': 1, 'half': 1, 'sums': 19, 'middle': 20, 'wide': 0, 'lateend': 1}
 
 
 class Box:

time: 358 us -> 356 us (level)
  local copies, waits for them, and re-layouts: 40.9 us -> 32.3 us
  waiting for transfers between devices: 113 us -> 121 us
  other arithmetic: 18.4 us -> 24.2 us
  starting transfers between devices: 85.9 us -> 80.2 us
    ppermute x10, waiting for transfers between devices: 14.3 us -> 29.1 us  [body(): near = lambda value: lax.ppermute(value, 'mp', flip(members, 1))]
    pallas_call x1, Pallas kernels: 22.9 us -> 10.9 us  [weigh(): pl.pallas_call(weigh_kernel, in_specs=[in_smem()] + [in_vmem()] * (2 * le...]
    pallas_call x2, Pallas kernels: 18.7 us -> 30.3 us  [feed(): pl.pallas_call(functools.partial(feed_kernel, len(pieces)), in_specs=[in_...]
    ppermute x9, waiting for transfers between devices: 58.6 us -> 49.2 us  [body(): far = lambda value: lax.ppermute(value, both, far_pairs)]
    unnamed x147 -> x137, local copies, waits for them, and re-layouts: 31.8 us -> 22.8 us
    ppermute x5, waiting for transfers between devices: 2.13 us -> 10.8 us  [add_up(): mate = lax.ppermute(values, axis, flip(size, bit))]
    ppermute x9, starting transfers between devices: 46.2 us -> 38.1 us  [body(): far = lambda value: lax.ppermute(value, both, far_pairs)]
    ppermute x2, waiting for transfers between devices: 5.62 us -> 0.01 us  [handed(): lax.ppermute(value, both, hand_pairs)]
  transfers between devices with their start and end apart: 57 -> 57, of which waited for: 23 -> 23; matrix products, arithmetic and copies ran while one was open for 8% -> 9% of each run, Pallas kernels for 23% -> 23%
where the time goes in v1:
time: 356 us; the launch traced here: 352 us
  waiting for transfers between devices  121 us (34%)
  Pallas kernels  90.6 us (25%)
  starting transfers between devices  80.2 us (23%)
  local copies, waits for them, and re-layouts  32.3 us (9%)
  other arithmetic  24.2 us (7%)
    ppermute x9, waiting for transfers between devices, body(): far = lambda value: lax.ppermute(value, both, far_pairs)  49.2 us
    ppermute x9, starting transfers between devices, body(): far = lambda value: lax.ppermute(value, both, far_pairs)  38.1 us
    pallas_call x2, Pallas kernels, feed(): pl.pallas_call(functools.partial(feed_kernel, len(pieces)), in_specs=[in_...  30.3 us
    ppermute x10, waiting for transfers between devices, body(): near = lambda value: lax.ppermute(value, 'mp', flip(members, 1))  29.1 us
    unnamed x137, local copies, waits for them, and re-layouts  22.8 us
    ppermute x6, waiting for transfers between devices, spread(): lax.ppermute(value, both, away_pairs(block))  20.7 us
    pallas_call x1, Pallas kernels, attend_back(): pl.pallas_call(attend_back_kernel, out_shape=shaped((rows, 3 * width), LO...  17.4 us
    ppermute x6, starting transfers between devices, spread(): lax.ppermute(value, both, away_pairs(block))  17.4 us
  transfers between devices with their start and end apart: 57, of which 23 were waited for; matrix products, arithmetic and copies ran while one was open for 9% of the time, Pallas kernels for 23%

profile of v1, /device:TPU:1, one launch (start us, length us, event | category | flops | bytes accessed | tf_op | source)
XLA Modules:
  0.0 351.8 jit_solution(11967415956422729616)
XLA Ops:
  0.6 5.6 %collective-permute-start = (bf16[384,1024]{1,0:T(8,128)(2,1)}, bf16[384,1024]{1,0:T(8,128)(2,1)S(1)}, u32[]{:S(2)}, u32[]{:S(2)}) collective-permute-start(bf16[384,1024]{1,0:T(8,128)(2,1)} %param.15), channel_id=1, source_target_pairs={{4,2},{5,3},{2,4},{3,5},{12,10},{13,11},{10,12},{11,13},{20,18},{2... | collective-permute-start | bytes 2359304 | tf_op jit(solution)/shard_map/ppermute | solution.py:636
  8.3 1.9 collective-permute-start.1
  12.7 4.5 %collective-permute-start.2 = (bf16[256,1024]{1,0:T(8,128)(2,1)S(1)}, bf16[256,1024]{1,0:T(8,128)(2,1)}, u32[]{:S(2)}, u32[]{:S(2)}) collective-permute-start(bf16[256,1024]{1,0:T(8,128)(2,1)S(1)} %pad_maximum_fusion.2), channel_id=1, source_target_pairs={{4,2},{5,3},{2,4},{3,5},{12,10},{13,11},{10,12},{11,13},{20,18},{2... | collective-permute-start | bytes 1572872 | tf_op jit(solution)/shard_map/first/ppermute | solution.py:636
  17.3 12.1 %collective-permute-done.1 = f32[16,128]{1,0:T(8,128)S(1)} collective-permute-done((f32[16,128]{1,0:T(8,128)S(1)}, f32[16,128]{1,0:T(8,128)S(1)}, u32[]{:S(2)}, u32[]{:S(2)}) %collective-permute-start.1) | collective-permute-done | bytes 8224 | tf_op jit(solution)/shard_map/notes/ppermute | solution.py:636
  30.5 5.6 %collective-permute-done.2.refs_0_ = bf16[256,1024]{1,0:T(8,128)(2,1)} collective-permute-done((bf16[256,1024]{1,0:T(8,128)(2,1)S(1)}, bf16[256,1024]{1,0:T(8,128)(2,1)}, u32[]{:S(2)}, u32[]{:S(2)}) %collective-permute-start.2) | collective-permute-done | bytes 524320 | tf_op jit(solution)/shard_map/first/ppermute | solution.py:636
  36.4 3.1 collective-permute-start.5
  39.5 3.1 collective-permute-start.6
  42.7 2.1 collective-permute-start.7
  47.9 6.5 %collective-permute-start.9 = (bf16[512,1024]{1,0:T(8,128)(2,1)}, bf16[512,1024]{1,0:T(8,128)(2,1)}, u32[]{:S(2)}, u32[]{:S(2)}) collective-permute-start(bf16[512,1024]{1,0:T(8,128)(2,1)} %pad_maximum_fusion), channel_id=1, source_target_pairs={{4,2},{5,3},{2,4},{3,5},{12,10},{13,11},{10,12},{11,13},{20,18},{2... | collective-permute-start | bytes 3145736 | tf_op jit(solution)/shard_map/second/ppermute | solution.py:636
  65.0 5.0 %open_up.1 = (bf16[384,768]{1,0:T(8,128)(2,1)S(1)}, bf16[384,768]{1,0:T(8,128)(2,1)S(1)}, bf16[384,768]{1,0:T(8,128)(2,1)S(1)}, bf16[384,768]{1,0:T(8,128)(2,1)S...) custom-call(s32[4]{0:T(128)S(1)} %pad_add_fusion.place_ref, f32[1,768]{1,0:T(1,128)S(1)} %copy-done.39, ...), custom_call_target="tpu_custom_call" | custom-call | flops 2415919104 | bytes 4194304 | tf_op jit(solution)/shard_map/open_up/pallas_call | solution.py:114
  71.1 6.9 %collective-permute-done.9.refs_0_ = bf16[512,1024]{1,0:T(8,128)(2,1)} collective-permute-done((bf16[512,1024]{1,0:T(8,128)(2,1)}, bf16[512,1024]{1,0:T(8,128)(2,1)}, u32[]{:S(2)}, u32[]{:S(2)}) %collective-permute-start.9) | collective-permute-done | bytes 1048608 | tf_op jit(solution)/shard_map/second/ppermute | solution.py:636
  78.0 5.1 %collective-permute-start.16 = (bf16[384,1024]{1,0:T(8,128)(2,1)S(1)}, bf16[384,1024]{1,0:T(8,128)(2,1)S(1)}, u32[]{:S(2)}, u32[]{:S(2)}) collective-permute-start(bf16[384,1024]{1,0:T(8,128)(2,1)S(1)} %copy-done.57), channel_id=1, source_target_pairs={{4,2},{5,3},{2,4},{3,5},{12,10},{13,11},{10,12},{11,13},{20,18},{2... | collective-permute-start | bytes 2359304 | tf_op jit(solution)/shard_map/cotangent/ppermute | solution.py:636
  83.1 11.1 %attend.1 = (bf16[256,1536]{1,0:T(8,128)(2,1)S(1)}, f32[8,1536]{1,0:T(8,128)S(1)}, bf16[384,256]{1,0:T(8,128)(2,1)S(1)}, bf16[384,256]{1,0:T(8,128)(2,1)S(1)}, b...) custom-call(s32[4]{0:T(128)S(1)} %pad_add_fusion.place_ref, bf16[384,768]{1,0:T(8,128)(2,1)S(1)} %get-tuple-element.134.refs_0_, ...), custom_call_target="tpu_custom_call" | custom-call | flops 9663676416 | bytes 3145728 | tf_op jit(solution)/shard_map/attend/pallas_call | solution.py:190
  96.6 8.3 %collective-permute-done.12.refs_1_ = bf16[384,256]{1,0:T(8,128)(2,1)S(1)} collective-permute-done((bf16[384,256]{1,0:T(8,128)(2,1)S(1)}, bf16[384,256]{1,0:T(8,128)(2,1)S(1)}, u32[]{:S(2)}, u32[]{:S(2)}) %collective-permute-start.12) | collective-permute-done | bytes 196640 | tf_op jit(solution)/shard_map/ppermute | solution.py:638
  104.9 3.9 %collective-permute-start.18 = (bf16[512,1024]{1,0:T(8,128)(2,1)}, bf16[512,1024]{1,0:T(8,128)(2,1)S(1)}, u32[]{:S(2)}, u32[]{:S(2)}) collective-permute-start(bf16[512,1024]{1,0:T(8,128)(2,1)} %collective-permute-done.9.refs_0_), channel_id=1, source_target_pairs={{4,12},{5,13},{2,10},{3,11},{12,4},{13,5},{10,2},{11,3},{20,28},{2... | collective-permute-start | bytes 3145736 | tf_op jit(solution)/shard_map/seconds/ppermute | solution.py:647
  108.8 3.1 collective-permute-start.19
  111.9 2.0 collective-permute-start.20
  116.2 5.2 %collective-permute-done.18.refs_1_ = bf16[512,1024]{1,0:T(8,128)(2,1)S(1)} collective-permute-done((bf16[512,1024]{1,0:T(8,128)(2,1)}, bf16[512,1024]{1,0:T(8,128)(2,1)S(1)}, u32[]{:S(2)}, u32[]{:S(2)}) %collective-permute-start.18) | collective-permute-done | bytes 1048608 | tf_op jit(solution)/shard_map/seconds/ppermute | solution.py:647
  121.4 14.6 %collective-permute-done.19.refs_2_ = bf16[512,1024]{1,0:T(8,128)(2,1)S(1)} collective-permute-done((bf16[512,1024]{1,0:T(8,128)(2,1)}, bf16[512,1024]{1,0:T(8,128)(2,1)S(1)}, u32[]{:S(2)}, u32[]{:S(2)}) %collective-permute-start.19) | collective-permute-done | bytes 1048608 | tf_op jit(solution)/shard_map/seconds/ppermute | solution.py:647
  136.1 21.6 %feed.2 = (bf16[768,1024]{1,0:T(8,128)(2,1)S(1)}, bf16[768,1024]{1,0:T(8,128)(2,1)S(1)}, f32[1,1024]{1,0:T(1,128)S(1)}, f32[384,1024]{1,0:T(8,128)S(1)}, f32[384...) custom-call(s32[4]{0:T(128)S(1)} %pad_add_fusion.place_ref, bf16[384,1024]{1,0:T(8,128)(2,1)S(1)} %get-tuple-element.171.x_one.refs_0_, ...), custom_call_target="tpu_custom_call" | custom-call | flops 6442450944 | bytes 4194304 | tf_op jit(solution)/shard_map/feed/pallas_call | solution.py:385
  164.6 8.7 %feed.3 = (bf16[768,1024]{1,0:T(8,128)(2,1)S(1)}, bf16[768,1024]{1,0:T(8,128)(2,1)S(1)}, f32[1,1024]{1,0:T(1,128)S(1)}, bf16[384,1024]{1,0:T(8,128)(2,1)S(1)}, b...) custom-call(s32[4]{0:T(128)S(1)} %pad_add_fusion.place_ref, ...), custom_call_target="tpu_custom_call" | custom-call | flops 6442450944 | bytes 4194304 | tf_op jit(solution)/shard_map/feed/pallas_call | solution.py:385
  174.5 3.0 collective-permute-done.26
  177.6 1.8 add_convert_fusion.4
  181.3 10.9 %weigh.1 = (bf16[2,256,1024]{2,1,0:T(8,128)(2,1)S(1)}, bf16[2,256,1024]{2,1,0:T(8,128)(2,1)}, bf16[2,256,1024]{2,1,0:T(8,128)(2,1)S(1)}, bf16[2,256,1024]{2,1,0:T(8,128)(2,1)}) custom-call(s32[4]{0:T(128)S(1)} %pad_add_fusion.place_ref, bf16[384,1024]{1,0:T(8,128)(2,1)S(1)} %get-tuple-element.171.x_one.refs_0_, ...), custom_call_target="tpu_custom_call" | custom-call | flops 6442450944 | bytes 16777216 | tf_op jit(solution)/shard_map/weigh/pallas_call | solution.py:454
  197.7 2.1 turn.1.turned_ref
  200.3 3.9 %unproject.1 = (bf16[384,1024]{1,0:T(8,128)(2,1)S(1)}, f32[384,1024]{1,0:T(8,128)S(1)}, f32[8,1024]{1,0:T(8,128)S(1)}, bf16[384,256]{1,0:T(8,128)(2,1)S(1)}, bf1...) custom-call(f32[384,1024]{1,0:T(8,128)S(1)} %copy-done.15, ...), custom_call_target="tpu_custom_call" | custom-call | flops 805306368 | bytes 9175040 | tf_op jit(solution)/shard_map/unproject/pallas_call | solution.py:420
  207.2 8.7 %collective-permute-done.32 = bf16[384,1024]{1,0:T(8,128)(2,1)} collective-permute-done((bf16[384,1024]{1,0:T(8,128)(2,1)}, bf16[384,1024]{1,0:T(8,128)(2,1)}, u32[]{:S(2)}, u32[]{:S(2)}) %collective-permute-start.32) | collective-permute-done | bytes 786464 | tf_op jit(solution)/shard_map/out/ppermute | solution.py:638
  216.0 2.9 collective-permute-start.31
  220.1 4.5 %collective-permute-done.31.refs_7_ = bf16[384,256]{1,0:T(8,128)(2,1)S(1)} collective-permute-done((bf16[384,256]{1,0:T(8,128)(2,1)S(1)}, bf16[384,256]{1,0:T(8,128)(2,1)S(1)}, u32[]{:S(2)}, u32[]{:S(2)}) %collective-permute-start.31) | collective-permute-done | bytes 196640 | tf_op jit(solution)/shard_map/ppermute | solution.py:639
  226.2 2.0 add_convert_fusion.3
  228.3 1.9 add_convert_fusion
  233.6 5.2 %collective-permute-start.39 = (bf16[384,1024]{1,0:T(8,128)(2,1)S(1)}, bf16[384,1024]{1,0:T(8,128)(2,1)S(1)}, u32[]{:S(2)}, u32[]{:S(2)}) collective-permute-start(bf16[384,1024]{1,0:T(8,128)(2,1)S(1)} %add_convert_fusion.3), channel_id=1, source_target_pairs={{4,2},{5,3},{2,4},{3,5},{12,10},{13,11},{10,12},{11,13},{20,18},{2... | collective-permute-start | bytes 2359304 | tf_op jit(solution)/shard_map/output/ppermute | solution.py:636
  238.8 17.4 %attend_back.1.projected_ref = bf16[1536,768]{1,0:T(8,128)(2,1)S(1)} custom-call(s32[4]{0:T(128)S(1)} %pad_add_fusion.place_ref, bf16[384,768]{1,0:T(8,128)(2,1)S(1)} %copy-done.45, bf16[384,768]{1,0:T(8,128)(2,1)S(1)} %copy-done.47, bf16[384,768]{1,0:T(8,128)(2,1)S(1)} %copy-done.49, bf16[384,768]{1,0:T(8,128)(2,1)S(1)} %copy-done.51, ...), custom_call_target="tpu_custom_call" | custom-call | flops 24159191040 | bytes 7864320 | tf_op jit(solution)/shard_map/attend_back/pallas_call | solution.py:300
  258.6 1.9 collective-permute-start.55
  260.7 2.6 share.1
  264.8 5.8 %weigh_late.1 = (bf16[2,256,512]{2,1,0:T(8,128)(2,1)S(1)}, bf16[2,256,512]{2,1,0:T(8,128)(2,1)}, bf16[2,256,512]{2,1,0:T(8,128)(2,1)S(1)}, bf16[2,256,512]{2,1,0...) custom-call(s32[4]{0:T(128)S(1)} %pad_add_fusion.place_ref, bf16[1024,1536]{1,0:T(8,128)(2,1)S(1)} %turn.1.turned_ref, ...), custom_call_target="tpu_custom_call" | custom-call | flops 3221225472 | bytes 9437184 | tf_op jit(solution)/shard_map/weigh_late/pallas_call | solution.py:515
  272.8 2.1 broadcast_select_fusion.1
  276.7 3.4 convert_add_fusion
  281.5 2.7 collective-permute-start.41
  285.6 4.0 %collective-permute-done.46 = f32[96,128]{1,0:T(8,128)S(1)} collective-permute-done((f32[96,128]{1,0:T(8,128)S(1)}, f32[96,128]{1,0:T(8,128)S(1)}, u32[]{:S(2)}, u32[]{:S(2)}) %collective-permute-start.46) | collective-permute-done | bytes 49184 | tf_op jit(solution)/shard_map/ppermute | solution.py:559
  293.4 10.9 %collective-permute-done.41 = bf16[384,1024]{1,0:T(8,128)(2,1)} collective-permute-done((bf16[384,1024]{1,0:T(8,128)(2,1)}, bf16[384,1024]{1,0:T(8,128)(2,1)}, u32[]{:S(2)}, u32[]{:S(2)}) %collective-permute-start.41) | collective-permute-done | bytes 786464 | tf_op jit(solution)/shard_map/ppermute | solution.py:638
  306.9 1.9 fusion.15
  309.4 2.7 collective-permute-done.51
  314.1 2.5 collective-permute-done.52
  316.8 3.9 %collective-permute-start.53 = (bf16[128,1024]{1,0:T(8,128)(2,1)S(1)}, bf16[128,1024]{1,0:T(8,128)(2,1)S(1)}, u32[]{:S(2)}, u32[]{:S(2)}) collective-permute-start(bf16[128,1024]{1,0:T(8,128)(2,1)S(1)} %get-tuple-element.278), channel_id=1, source_target_pairs={{4,2},{5,3},{2,4},{3,5},{12,10},{13,11},{10,12},{11,13},{20,18},{2... | collective-permute-start | bytes 786440 | tf_op jit(solution)/shard_map/latehand/ppermute | solution.py:636
  320.8 3.5 collective-permute-start.50
  326.1 13.3 %collective-permute-done.53 = bf16[128,1024]{1,0:T(8,128)(2,1)S(1)} collective-permute-done((bf16[128,1024]{1,0:T(8,128)(2,1)S(1)}, bf16[128,1024]{1,0:T(8,128)(2,1)S(1)}, u32[]{:S(2)}, u32[]{:S(2)}) %collective-permute-start.53) | collective-permute-done | bytes 262176 | tf_op jit(solution)/shard_map/latehand/ppermute | solution.py:636
  341.5 9.2 %collective-permute-done.50 = bf16[384,1024]{1,0:T(8,128)(2,1)S(1)} collective-permute-done((bf16[384,1024]{1,0:T(8,128)(2,1)S(1)}, bf16[384,1024]{1,0:T(8,128)(2,1)S(1)}, u32[]{:S(2)}, u32[]{:S(2)}) %collective-permute-start.50) | collective-permute-done | bytes 786464 | tf_op jit(solution)/shard_map/ppermute | solution.py:636
  (287 shorter events, 73.5 us)
Async XLA Ops:
  0.6 28.8 %collective-permute-start = (bf16[384,1024]{1,0:T(8,128)(2,1)}, bf16[384,1024]{1,0:T(8,128)(2,1)S(1)}, u32[]{:S(2)}, u32[]{:S(2)}) collective-permute-start(bf16[384,1024]{1,0:T(8,128)(2,1)} %param.15), channel_id=1, source_target_pairs={{4,2},{5,3},{2,4},{3,5},{12,10},{13,11},{10,12},{11,13},{20,18},{2... | collective-permute-start | bytes 2359304 | tf_op jit(solution)/shard_map/ppermute | solution.py:636
  8.3 21.1 %collective-permute-start.1 = (f32[16,128]{1,0:T(8,128)S(1)}, f32[16,128]{1,0:T(8,128)S(1)}, u32[]{:S(2)}, u32[]{:S(2)}) collective-permute-start(f32[16,128]{1,0:T(8,128)S(1)} %fusion.20), channel_id=1, source_target_pairs={{4,2},{5,3},{2,4},{3,5},{12,10},{13,11},{10,12},{11,13},{20,18},{2... | collective-permute-start | bytes 24584 | tf_op jit(solution)/shard_map/notes/ppermute | solution.py:636
  12.7 23.3 %collective-permute-start.2 = (bf16[256,1024]{1,0:T(8,128)(2,1)S(1)}, bf16[256,1024]{1,0:T(8,128)(2,1)}, u32[]{:S(2)}, u32[]{:S(2)}) collective-permute-start(bf16[256,1024]{1,0:T(8,128)(2,1)S(1)} %pad_maximum_fusion.2), channel_id=1, source_target_pairs={{4,2},{5,3},{2,4},{3,5},{12,10},{13,11},{10,12},{11,13},{20,18},{2... | collective-permute-start | bytes 1572872 | tf_op jit(solution)/shard_map/first/ppermute | solution.py:636
  36.1 20.8 %collective-permute-start.3 = (bf16[384,1024]{1,0:T(8,128)(2,1)S(1)}, bf16[384,1024]{1,0:T(8,128)(2,1)S(1)}, u32[]{:S(2)}, u32[]{:S(2)}) collective-permute-start(bf16[384,1024]{1,0:T(8,128)(2,1)S(1)} %fusion.6.refs_4_.refs_0_), channel_id=1, source_target_pairs={{0,1},{1,0},{2,3},{3,2},{4,5},{5,4},{6,7},{7,6},{8,9},{9,8},{10,11... | collective-permute-start | bytes 2359304 | tf_op jit(solution)/shard_map/ppermute | solution.py:638
  36.4 20.5 %collective-permute-start.4 = (bf16[384,1024]{1,0:T(8,128)(2,1)S(1)}, bf16[384,1024]{1,0:T(8,128)(2,1)S(1)}, u32[]{:S(2)}, u32[]{:S(2)}) collective-permute-start(bf16[384,1024]{1,0:T(8,128)(2,1)S(1)} %fusion.6.refs_4_.refs_0_), channel_id=1, source_target_pairs={{0,4},{4,0},{8,12},{12,8},{16,20},{20,16},{24,28},{28,24},{1,5},{5... | collective-permute-start | bytes 2359304 | tf_op jit(solution)/shard_map/ppermute | solution.py:637
  36.4 10.7 %collective-permute-start.5 = (bf16[256,1024]{1,0:T(8,128)(2,1)}, bf16[256,1024]{1,0:T(8,128)(2,1)S(1)}, u32[]{:S(2)}, u32[]{:S(2)}) collective-permute-start(bf16[256,1024]{1,0:T(8,128)(2,1)} %collective-permute-done.2.refs_0_), channel_id=1, source_target_pairs={{4,12},{5,13},{2,10},{3,11},{12,4},{13,5},{10,2},{11,3},{20,28},{2... | collective-permute-start | bytes 1572872 | tf_op jit(solution)/shard_map/pieces/ppermute | solution.py:647
  39.5 15.8 %collective-permute-start.6 = (bf16[256,1024]{1,0:T(8,128)(2,1)}, bf16[256,1024]{1,0:T(8,128)(2,1)S(1)}, u32[]{:S(2)}, u32[]{:S(2)}) collective-permute-start(bf16[256,1024]{1,0:T(8,128)(2,1)} %collective-permute-done.2.refs_0_), channel_id=1, source_target_pairs={{4,20},{5,21},{2,18},{3,19},{12,28},{13,29},{10,26},{11,27},{20,4}... | collective-permute-start | bytes 1572872 | tf_op jit(solution)/shard_map/pieces/ppermute | solution.py:647
  42.7 13.4 %collective-permute-start.7 = (bf16[256,1024]{1,0:T(8,128)(2,1)}, bf16[256,1024]{1,0:T(8,128)(2,1)S(1)}, u32[]{:S(2)}, u32[]{:S(2)}) collective-permute-start(bf16[256,1024]{1,0:T(8,128)(2,1)} %collective-permute-done.2.refs_0_), channel_id=1, source_target_pairs={{4,28},{5,29},{2,26},{3,27},{12,20},{13,21},{10,18},{11,19},{20,12... | collective-permute-start | bytes 1572872 | tf_op jit(solution)/shard_map/pieces/ppermute | solution.py:647
  47.9 30.1 %collective-permute-start.9 = (bf16[512,1024]{1,0:T(8,128)(2,1)}, bf16[512,1024]{1,0:T(8,128)(2,1)}, u32[]{:S(2)}, u32[]{:S(2)}) collective-permute-start(bf16[512,1024]{1,0:T(8,128)(2,1)} %pad_maximum_fusion), channel_id=1, source_target_pairs={{4,2},{5,3},{2,4},{3,5},{12,10},{13,11},{10,12},{11,13},{20,18},{2... | collective-permute-start | bytes 3145736 | tf_op jit(solution)/shard_map/second/ppermute | solution.py:636
  78.0 16.3 %collective-permute-start.10 = (bf16[1024,256]{1,0:T(8,128)(2,1)S(1)}, bf16[1024,256]{1,0:T(8,128)(2,1)S(1)}, u32[]{:S(2)}, u32[]{:S(2)}) collective-permute-start(bf16[1024,256]{1,0:T(8,128)(2,1)S(1)} %get-tuple-element.144.refs_4_.refs_0_), channel_id=1, source_target_pairs={{0,1},{1,0},{2,3},{3,2},{4,5},{5,4},{6,7},{7,6},{8,9},{9,8},{10,11... | collective-permute-start | bytes 1572872 | tf_op jit(solution)/shard_map/outs/ppermute | solution.py:638
  78.0 16.4 %collective-permute-start.11 = (bf16[1024,256]{1,0:T(8,128)(2,1)S(1)}, bf16[1024,256]{1,0:T(8,128)(2,1)S(1)}, u32[]{:S(2)}, u32[]{:S(2)}) collective-permute-start(bf16[1024,256]{1,0:T(8,128)(2,1)S(1)} %get-tuple-element.144.refs_4_.refs_0_), channel_id=1, source_target_pairs={{0,4},{4,0},{8,12},{12,8},{16,20},{20,16},{24,28},{28,24},{1,5},{5... | collective-permute-start | bytes 1572872 | tf_op jit(solution)/shard_map/outs/ppermute | solution.py:637
  78.0 37.5 %collective-permute-start.16 = (bf16[384,1024]{1,0:T(8,128)(2,1)S(1)}, bf16[384,1024]{1,0:T(8,128)(2,1)S(1)}, u32[]{:S(2)}, u32[]{:S(2)}) collective-permute-start(bf16[384,1024]{1,0:T(8,128)(2,1)S(1)} %copy-done.57), channel_id=1, source_target_pairs={{4,2},{5,3},{2,4},{3,5},{12,10},{13,11},{10,12},{11,13},{20,18},{2... | collective-permute-start | bytes 2359304 | tf_op jit(solution)/shard_map/cotangent/ppermute | solution.py:636
  94.4 19.6 %collective-permute-start.15 = (bf16[1024,256]{1,0:T(8,128)(2,1)S(1)}, bf16[1024,256]{1,0:T(8,128)(2,1)S(1)}, u32[]{:S(2)}, u32[]{:S(2)}) collective-permute-start(bf16[1024,256]{1,0:T(8,128)(2,1)S(1)} %collective-permute-done.10.refs_5_.refs_1_), channel_id=1, source_target_pairs={{0,4},{4,0},{8,12},{12,8},{16,20},{20,16},{24,28},{28,24},{1,5},{5... | collective-permute-start | bytes 1572872 | tf_op jit(solution)/shard_map/last/ppermute | solution.py:637
  94.5 10.4 %collective-permute-start.12 = (bf16[384,256]{1,0:T(8,128)(2,1)S(1)}, bf16[384,256]{1,0:T(8,128)(2,1)S(1)}, u32[]{:S(2)}, u32[]{:S(2)}) collective-permute-start(bf16[384,256]{1,0:T(8,128)(2,1)S(1)} %get-tuple-element.145), channel_id=1, source_target_pairs={{0,1},{1,0},{2,3},{3,2},{4,5},{5,4},{6,7},{7,6},{8,9},{9,8},{10,11... | collective-permute-start | bytes 589832 | tf_op jit(solution)/shard_map/ppermute | solution.py:638
  94.5 14.2 %collective-permute-start.13 = (bf16[384,256]{1,0:T(8,128)(2,1)S(1)}, bf16[384,256]{1,0:T(8,128)(2,1)S(1)}, u32[]{:S(2)}, u32[]{:S(2)}) collective-permute-start(bf16[384,256]{1,0:T(8,128)(2,1)S(1)} %get-tuple-element.146), channel_id=1, source_target_pairs={{0,4},{4,0},{8,12},{12,8},{16,20},{20,16},{24,28},{28,24},{1,5},{5... | collective-permute-start | bytes 589832 | tf_op jit(solution)/shard_map/ppermute | solution.py:637
  95.0 16.9 %collective-permute-start.14 = (bf16[384,256]{1,0:T(8,128)(2,1)S(1)}, bf16[384,256]{1,0:T(8,128)(2,1)S(1)}, u32[]{:S(2)}, u32[]{:S(2)}) collective-permute-start(bf16[384,256]{1,0:T(8,128)(2,1)S(1)} %get-tuple-element.147), channel_id=1, source_target_pairs={{0,5},{1,4},{2,7},{3,6},{4,1},{5,0},{6,3},{7,2},{8,13},{9,12},{10,... | collective-permute-start | bytes 589832 | tf_op jit(solution)/shard_map/ppermute | solution.py:639
  104.9 16.6 %collective-permute-start.18 = (bf16[512,1024]{1,0:T(8,128)(2,1)}, bf16[512,1024]{1,0:T(8,128)(2,1)S(1)}, u32[]{:S(2)}, u32[]{:S(2)}) collective-permute-start(bf16[512,1024]{1,0:T(8,128)(2,1)} %collective-permute-done.9.refs_0_), channel_id=1, source_target_pairs={{4,12},{5,13},{2,10},{3,11},{12,4},{13,5},{10,2},{11,3},{20,28},{2... | collective-permute-start | bytes 3145736 | tf_op jit(solution)/shard_map/seconds/ppermute | solution.py:647
  108.8 27.3 %collective-permute-start.19 = (bf16[512,1024]{1,0:T(8,128)(2,1)}, bf16[512,1024]{1,0:T(8,128)(2,1)S(1)}, u32[]{:S(2)}, u32[]{:S(2)}) collective-permute-start(bf16[512,1024]{1,0:T(8,128)(2,1)} %collective-permute-done.9.refs_0_), channel_id=1, source_target_pairs={{4,20},{5,21},{2,18},{3,19},{12,28},{13,29},{10,26},{11,27},{20,4}... | collective-permute-start | bytes 3145736 | tf_op jit(solution)/shard_map/seconds/ppermute | solution.py:647
  111.9 24.1 %collective-permute-start.20 = (bf16[512,1024]{1,0:T(8,128)(2,1)}, bf16[512,1024]{1,0:T(8,128)(2,1)S(1)}, u32[]{:S(2)}, u32[]{:S(2)}) collective-permute-start(bf16[512,1024]{1,0:T(8,128)(2,1)} %collective-permute-done.9.refs_0_), channel_id=1, source_target_pairs={{4,28},{5,29},{2,26},{3,27},{12,20},{13,21},{10,18},{11,19},{20,12... | collective-permute-start | bytes 3145736 | tf_op jit(solution)/shard_map/seconds/ppermute | solution.py:647
  115.5 20.6 %collective-permute-start.17 = (bf16[384,1024]{1,0:T(8,128)(2,1)S(1)}, bf16[384,1024]{1,0:T(8,128)(2,1)S(1)}, u32[]{:S(2)}, u32[]{:S(2)}) collective-permute-start(bf16[384,1024]{1,0:T(8,128)(2,1)S(1)} %get-tuple-element.171.x_one.refs_0_), channel_id=1, source_target_pairs={{0,4},{4,0},{8,12},{12,8},{16,20},{20,16},{24,28},{28,24},{1,5},{5... | collective-permute-start | bytes 2359304 | tf_op jit(solution)/shard_map/ppermute | solution.py:637
  115.7 20.4 %collective-permute-start.21 = (bf16[384,1024]{1,0:T(8,128)(2,1)S(1)}, bf16[384,1024]{1,0:T(8,128)(2,1)S(1)}, u32[]{:S(2)}, u32[]{:S(2)}) collective-permute-start(bf16[384,1024]{1,0:T(8,128)(2,1)S(1)} %broadcast_select_fusion.2.g_one.refs_4_.cotangent_ref), channel_id=1, source_target_pairs={{0,4},{4,0},{8,12},{12,8},{16,20},{20,16},{24,28},{28,24},{1,5},{5... | collective-permute-start | bytes 2359304 | tf_op jit(solution)/shard_map/ppermute | solution.py:637
  121.4 39.8 %collective-permute-start.23 = (bf16[384,1024]{1,0:T(8,128)(2,1)S(1)}, bf16[384,1024]{1,0:T(8,128)(2,1)S(1)}, u32[]{:S(2)}, u32[]{:S(2)}) collective-permute-start(bf16[384,1024]{1,0:T(8,128)(2,1)S(1)} %broadcast_select_fusion.2.g_one.refs_4_.cotangent_ref), channel_id=1, source_target_pairs={{0,1},{1,0},{2,3},{3,2},{4,5},{5,4},{6,7},{7,6},{8,9},{9,8},{10,11... | collective-permute-start | bytes 2359304 | tf_op jit(solution)/shard_map/cotnear/ppermute | solution.py:638
  136.1 25.2 %collective-permute-start.22 = (bf16[384,1024]{1,0:T(8,128)(2,1)S(1)}, bf16[384,1024]{1,0:T(8,128)(2,1)S(1)}, u32[]{:S(2)}, u32[]{:S(2)}) collective-permute-start(bf16[384,1024]{1,0:T(8,128)(2,1)S(1)} %get-tuple-element.171.x_one.refs_0_), channel_id=1, source_target_pairs={{0,1},{1,0},{2,3},{3,2},{4,5},{5,4},{6,7},{7,6},{8,9},{9,8},{10,11... | collective-permute-start | bytes 2359304 | tf_op jit(solution)/shard_map/secnear/ppermute | solution.py:638
  179.4 20.8 %collective-permute-start.28 = (bf16[768,1024]{1,0:T(8,128)(2,1)}, bf16[768,1024]{1,0:T(8,128)(2,1)}, u32[]{:S(2)}, u32[]{:S(2)}) collective-permute-start(bf16[768,1024]{1,0:T(8,128)(2,1)} %get-tuple-element.177), channel_id=1, source_target_pairs={{0,4},{4,0},{8,12},{12,8},{16,20},{20,16},{24,28},{28,24},{1,5},{5... | collective-permute-start | bytes 4718600 | tf_op jit(solution)/shard_map/two/ppermute | solution.py:637
  179.8 20.4 %collective-permute-start.27 = (bf16[384,1024]{1,0:T(8,128)(2,1)}, bf16[384,1024]{1,0:T(8,128)(2,1)}, u32[]{:S(2)}, u32[]{:S(2)}) collective-permute-start(bf16[384,1024]{1,0:T(8,128)(2,1)} %get-tuple-element.273), channel_id=1, source_target_pairs={{0,1},{1,0},{2,3},{3,2},{4,5},{5,4},{6,7},{7,6},{8,9},{9,8},{10,11... | collective-permute-start | bytes 2359304 | tf_op jit(solution)/shard_map/ppermute | solution.py:638
  181.2 34.7 %collective-permute-start.32 = (bf16[384,1024]{1,0:T(8,128)(2,1)}, bf16[384,1024]{1,0:T(8,128)(2,1)}, u32[]{:S(2)}, u32[]{:S(2)}) collective-permute-start(bf16[384,1024]{1,0:T(8,128)(2,1)} %get-tuple-element.272), channel_id=1, source_target_pairs={{0,1},{1,0},{2,3},{3,2},{4,5},{5,4},{6,7},{7,6},{8,9},{9,8},{10,11... | collective-permute-start | bytes 2359304 | tf_op jit(solution)/shard_map/out/ppermute | solution.py:638
  194.2 34.1 %collective-permute-start.33 = (bf16[2,256,1024]{2,1,0:T(8,128)(2,1)}, bf16[2,256,1024]{2,1,0:T(8,128)(2,1)}, u32[]{:S(2)}, u32[]{:S(2)}) collective-permute-start(bf16[2,256,1024]{2,1,0:T(8,128)(2,1)} %get-tuple-element.189), channel_id=1, source_target_pairs={{0,8},{4,12},{8,0},{12,4},{16,24},{20,28},{24,16},{28,20},{1,9},{5... | collective-permute-start | bytes 3145736 | tf_op jit(solution)/shard_map/fed/ppermute | solution.py:640
  194.2 34.1 %collective-permute-start.34 = (bf16[2,256,1024]{2,1,0:T(8,128)(2,1)}, bf16[2,256,1024]{2,1,0:T(8,128)(2,1)}, u32[]{:S(2)}, u32[]{:S(2)}) collective-permute-start(bf16[2,256,1024]{2,1,0:T(8,128)(2,1)} %get-tuple-element.190), channel_id=1, source_target_pairs={{0,16},{4,20},{8,24},{12,28},{16,0},{20,4},{24,8},{28,12},{1,17},{... | collective-permute-start | bytes 3145736 | tf_op jit(solution)/shard_map/fed/ppermute | solution.py:640
  204.2 15.9 %collective-permute-start.29 = (bf16[384,256]{1,0:T(8,128)(2,1)S(1)}, bf16[384,256]{1,0:T(8,128)(2,1)S(1)}, u32[]{:S(2)}, u32[]{:S(2)}) collective-permute-start(bf16[384,256]{1,0:T(8,128)(2,1)S(1)} %get-tuple-element.181), channel_id=1, source_target_pairs={{0,1},{1,0},{2,3},{3,2},{4,5},{5,4},{6,7},{7,6},{8,9},{9,8},{10,11... | collective-permute-start | bytes 589832 | tf_op jit(solution)/shard_map/ppermute | solution.py:638
  205.7 14.4 %collective-permute-start.30 = (bf16[384,256]{1,0:T(8,128)(2,1)S(1)}, bf16[384,256]{1,0:T(8,128)(2,1)S(1)}, u32[]{:S(2)}, u32[]{:S(2)}) collective-permute-start(bf16[384,256]{1,0:T(8,128)(2,1)S(1)} %get-tuple-element.182), channel_id=1, source_target_pairs={{0,4},{4,0},{8,12},{12,8},{16,20},{20,16},{24,28},{28,24},{1,5},{5... | collective-permute-start | bytes 589832 | tf_op jit(solution)/shard_map/ppermute | solution.py:637
  216.0 8.6 %collective-permute-start.31 = (bf16[384,256]{1,0:T(8,128)(2,1)S(1)}, bf16[384,256]{1,0:T(8,128)(2,1)S(1)}, u32[]{:S(2)}, u32[]{:S(2)}) collective-permute-start(bf16[384,256]{1,0:T(8,128)(2,1)S(1)} %get-tuple-element.183), channel_id=1, source_target_pairs={{0,5},{1,4},{2,7},{3,6},{4,1},{5,0},{6,3},{7,2},{8,13},{9,12},{10,... | collective-permute-start | bytes 589832 | tf_op jit(solution)/shard_map/ppermute | solution.py:639
  224.5 32.4 %collective-permute-start.35 = (bf16[384,1024]{1,0:T(8,128)(2,1)S(1)}, bf16[384,1024]{1,0:T(8,128)(2,1)S(1)}, u32[]{:S(2)}, u32[]{:S(2)}) collective-permute-start(bf16[384,1024]{1,0:T(8,128)(2,1)S(1)} %get-tuple-element.200.refs_0_), channel_id=1, source_target_pairs={{0,4},{4,0},{8,12},{12,8},{16,20},{20,16},{24,28},{28,24},{1,5},{5... | collective-permute-start | bytes 2359304 | tf_op jit(solution)/shard_map/low/ppermute | solution.py:637
  224.7 32.2 %collective-permute-start.36 = (bf16[384,1024]{1,0:T(8,128)(2,1)S(1)}, bf16[384,1024]{1,0:T(8,128)(2,1)S(1)}, u32[]{:S(2)}, u32[]{:S(2)}) collective-permute-start(bf16[384,1024]{1,0:T(8,128)(2,1)S(1)} %get-tuple-element.200.refs_0_), channel_id=1, source_target_pairs={{0,1},{1,0},{2,3},{3,2},{4,5},{5,4},{6,7},{7,6},{8,9},{9,8},{10,11... | collective-permute-start | bytes 2359304 | tf_op jit(solution)/shard_map/low/ppermute | solution.py:638
  230.3 25.9 %collective-permute-start.38 = (bf16[1,256,1024]{2,1,0:T(8,128)(2,1)S(1)}, bf16[1,256,1024]{2,1,0:T(8,128)(2,1)S(1)}, u32[]{:S(2)}, u32[]{:S(2)}) collective-permute-start(bf16[1,256,1024]{2,1,0:T(8,128)(2,1)S(1)} %slice.181), channel_id=1, source_target_pairs={{0,8},{4,12},{8,0},{12,4},{16,24},{20,28},{24,16},{28,20},{1,9},{5... | collective-permute-start | bytes 1572872 | tf_op jit(solution)/shard_map/fedrest/ppermute | solution.py:640
  232.2 24.0 %collective-permute-start.37 = (bf16[1,256,1024]{2,1,0:T(8,128)(2,1)S(1)}, bf16[1,256,1024]{2,1,0:T(8,128)(2,1)S(1)}, u32[]{:S(2)}, u32[]{:S(2)}) collective-permute-start(bf16[1,256,1024]{2,1,0:T(8,128)(2,1)S(1)} %slice.180), channel_id=1, source_target_pairs={{0,16},{4,20},{8,24},{12,28},{16,0},{20,4},{24,8},{28,12},{1,17},{... | collective-permute-start | bytes 1572872 | tf_op jit(solution)/shard_map/fedrest/ppermute | solution.py:640
  233.6 23.3 %collective-permute-start.39 = (bf16[384,1024]{1,0:T(8,128)(2,1)S(1)}, bf16[384,1024]{1,0:T(8,128)(2,1)S(1)}, u32[]{:S(2)}, u32[]{:S(2)}) collective-permute-start(bf16[384,1024]{1,0:T(8,128)(2,1)S(1)} %add_convert_fusion.3), channel_id=1, source_target_pairs={{4,2},{5,3},{2,4},{3,5},{12,10},{13,11},{10,12},{11,13},{20,18},{2... | collective-permute-start | bytes 2359304 | tf_op jit(solution)/shard_map/output/ppermute | solution.py:636
  258.6 22.9 %collective-permute-start.55 = (bf16[128,2048]{1,0:T(8,128)(2,1)}, bf16[128,2048]{1,0:T(8,128)(2,1)}, u32[]{:S(2)}, u32[]{:S(2)}) collective-permute-start(bf16[128,2048]{1,0:T(8,128)(2,1)} %get-tuple-element.276), channel_id=1, source_target_pairs={{4,2},{5,3},{2,4},{3,5},{12,10},{13,11},{10,12},{11,13},{20,18},{2... | collective-permute-start | bytes 1572872 | tf_op jit(solution)/shard_map/hand/ppermute | solution.py:636
  260.5 23.8 %collective-permute-start.56 = (bf16[128,2048]{1,0:T(8,128)(2,1)}, bf16[128,2048]{1,0:T(8,128)(2,1)}, u32[]{:S(2)}, u32[]{:S(2)}) collective-permute-start(bf16[128,2048]{1,0:T(8,128)(2,1)} %get-tuple-element.277), channel_id=1, source_target_pairs={{4,6},{5,7},{2,0},{3,1},{12,14},{13,15},{10,8},{11,9},{20,22},{21,... | collective-permute-start | bytes 1572872 | tf_op jit(solution)/shard_map/hand/ppermute | solution.py:742
  264.3 11.8 %collective-permute-start.40 = (bf16[768,1024]{1,0:T(8,128)(2,1)}, bf16[768,1024]{1,0:T(8,128)(2,1)}, u32[]{:S(2)}, u32[]{:S(2)}) collective-permute-start(bf16[768,1024]{1,0:T(8,128)(2,1)} %get-tuple-element.213), channel_id=1, source_target_pairs={{0,4},{4,0},{8,12},{12,8},{16,20},{20,16},{24,28},{28,24},{1,5},{5... | collective-permute-start | bytes 4718600 | tf_op jit(solution)/shard_map/ppermute | solution.py:637
  274.9 18.5 %collective-permute-start.43 = (bf16[2,256,512]{2,1,0:T(8,128)(2,1)}, bf16[2,256,512]{2,1,0:T(8,128)(2,1)S(1)}, u32[]{:S(2)}, u32[]{:S(2)}) collective-permute-start(bf16[2,256,512]{2,1,0:T(8,128)(2,1)} %get-tuple-element.218), channel_id=1, source_target_pairs={{0,8},{4,12},{8,0},{12,4},{16,24},{20,28},{24,16},{28,20},{1,9},{5... | collective-permute-start | bytes 1572872 | tf_op jit(solution)/shard_map/late/ppermute | solution.py:640
  275.9 17.5 %collective-permute-start.44 = (bf16[2,256,512]{2,1,0:T(8,128)(2,1)}, bf16[2,256,512]{2,1,0:T(8,128)(2,1)}, u32[]{:S(2)}, u32[]{:S(2)}) collective-permute-start(bf16[2,256,512]{2,1,0:T(8,128)(2,1)} %get-tuple-element.219), channel_id=1, source_target_pairs={{0,16},{4,20},{8,24},{12,28},{16,0},{20,4},{24,8},{28,12},{1,17},{... | collective-permute-start | bytes 1572872 | tf_op jit(solution)/shard_map/late/ppermute | solution.py:640
  276.1 13.5 %collective-permute-start.46 = (f32[96,128]{1,0:T(8,128)S(1)}, f32[96,128]{1,0:T(8,128)S(1)}, u32[]{:S(2)}, u32[]{:S(2)}) collective-permute-start(f32[96,128]{1,0:T(8,128)S(1)} %bitcast_add_fusion), channel_id=1, source_target_pairs={{0,8},{4,12},{8,0},{12,4},{16,24},{20,28},{24,16},{28,20},{1,9},{5... | collective-permute-start | bytes 147464 | tf_op jit(solution)/shard_map/ppermute | solution.py:559
  281.5 22.8 %collective-permute-start.41 = (bf16[384,1024]{1,0:T(8,128)(2,1)}, bf16[384,1024]{1,0:T(8,128)(2,1)}, u32[]{:S(2)}, u32[]{:S(2)}) collective-permute-start(bf16[384,1024]{1,0:T(8,128)(2,1)} %get-tuple-element.271), channel_id=1, source_target_pairs={{0,1},{1,0},{2,3},{3,2},{4,5},{5,4},{6,7},{7,6},{8,9},{9,8},{10,11... | collective-permute-start | bytes 2359304 | tf_op jit(solution)/shard_map/ppermute | solution.py:638
  305.5 11.1 %collective-permute-start.49 = (bf16[1,256,512]{2,1,0:T(8,128)(2,1)S(1)}, bf16[1,256,512]{2,1,0:T(8,128)(2,1)S(1)}, u32[]{:S(2)}, u32[]{:S(2)}) collective-permute-start(bf16[1,256,512]{2,1,0:T(8,128)(2,1)S(1)} %slice.187), channel_id=1, source_target_pairs={{0,8},{4,12},{8,0},{12,4},{16,24},{20,28},{24,16},{28,20},{1,9},{5... | collective-permute-start | bytes 786440 | tf_op jit(solution)/shard_map/laterest/ppermute | solution.py:640
  306.6 10.0 %collective-permute-start.48 = (bf16[1,256,512]{2,1,0:T(8,128)(2,1)S(1)}, bf16[1,256,512]{2,1,0:T(8,128)(2,1)S(1)}, u32[]{:S(2)}, u32[]{:S(2)}) collective-permute-start(bf16[1,256,512]{2,1,0:T(8,128)(2,1)S(1)} %slice.186), channel_id=1, source_target_pairs={{0,16},{4,20},{8,24},{12,28},{16,0},{20,4},{24,8},{28,12},{1,17},{... | collective-permute-start | bytes 786440 | tf_op jit(solution)/shard_map/laterest/ppermute | solution.py:640
  316.8 22.6 %collective-permute-start.53 = (bf16[128,1024]{1,0:T(8,128)(2,1)S(1)}, bf16[128,1024]{1,0:T(8,128)(2,1)S(1)}, u32[]{:S(2)}, u32[]{:S(2)}) collective-permute-start(bf16[128,1024]{1,0:T(8,128)(2,1)S(1)} %get-tuple-element.278), channel_id=1, source_target_pairs={{4,2},{5,3},{2,4},{3,5},{12,10},{13,11},{10,12},{11,13},{20,18},{2... | collective-permute-start | bytes 786440 | tf_op jit(solution)/shard_map/latehand/ppermute | solution.py:636
  320.7 18.7 %collective-permute-start.54 = (bf16[128,1024]{1,0:T(8,128)(2,1)S(1)}, bf16[128,1024]{1,0:T(8,128)(2,1)S(1)}, u32[]{:S(2)}, u32[]{:S(2)}) collective-permute-start(bf16[128,1024]{1,0:T(8,128)(2,1)S(1)} %get-tuple-element.279), channel_id=1, source_target_pairs={{4,6},{5,7},{2,0},{3,1},{12,14},{13,15},{10,8},{11,9},{20,22},{21,... | collective-permute-start | bytes 786440 | tf_op jit(solution)/shard_map/latehand/ppermute | solution.py:742
  320.8 29.9 %collective-permute-start.50 = (bf16[384,1024]{1,0:T(8,128)(2,1)S(1)}, bf16[384,1024]{1,0:T(8,128)(2,1)S(1)}, u32[]{:S(2)}, u32[]{:S(2)}) collective-permute-start(bf16[384,1024]{1,0:T(8,128)(2,1)S(1)} %fusion.11), channel_id=1, source_target_pairs={{4,2},{5,3},{2,4},{3,5},{12,10},{13,11},{10,12},{11,13},{20,18},{2... | collective-permute-start | bytes 2359304 | tf_op jit(solution)/shard_map/ppermute | solution.py:636
  (72 other events, 694.9 us)
